TPU v7x, 128 devices: a whole 4x4x4 slice. The times are simulated.
128 devices in a mesh: patch: 16 (over y, z), hidden: 8 (over x, core).
Axes of the slice: x: 4, y: 4, z: 4, core: 2. Of those that a mesh axis runs over, the one named last changes fastest.
Arguments:
- grid_latent: bfloat16 [49152, 512], P('patch'), may hold values from -6 to 6
- mesh_latent: bfloat16 [81920, 512], P('patch'), may hold values from -6 to 6
- edge_latent: bfloat16 [131072, 512], P('patch'), may hold values from -6 to 6
- senders: int32 [131072], P('patch'), may hold values from 0 to 49151, as said below
- receivers: int32 [131072], P('patch'), may hold values from 0 to 81919
- mesh_slot: int32 [81920], replicated, may hold values from 0 to 81919, as said below
- edge_counts: int32 [16], P('patch'), may hold values from 2730 to 8192, as said below
- w_edge: bfloat16 [512, 512], P(None, 'hidden'), may hold values from -0.25 to 0.25
- w_sender: bfloat16 [512, 512], P(None, 'hidden'), may hold values from -0.25 to 0.25
- w_receiver: bfloat16 [512, 512], P(None, 'hidden'), may hold values from -0.25 to 0.25
- edge_bias: float32 [512], P('hidden'), may hold values from -3 to 3
- w_edge_out: bfloat16 [512, 512], P('hidden'), may hold values from -0.25 to 0.25
- edge_out_bias: float32 [512], P('hidden'), may hold values from -3 to 3
- edge_gain: float32 [512], P('hidden'), may hold values from 0.25 to 1.75
- edge_shift: float32 [512], P('hidden'), may hold values from -2 to 2
- w_mesh_in: bfloat16 [512, 512], P(None, 'hidden'), may hold values from -0.25 to 0.25
- w_message_in: bfloat16 [512, 512], P(None, 'hidden'), may hold values from -0.25 to 0.25
- mesh_bias: float32 [512], P('hidden'), may hold values from -3 to 3
- w_mesh_out: bfloat16 [512, 512], P('hidden'), may hold values from -0.25 to 0.25
- mesh_out_bias: float32 [512], P('hidden'), may hold values from -3 to 3
- mesh_gain: float32 [512], P('hidden'), may hold values from 0.25 to 1.75
- mesh_shift: float32 [512], P('hidden'), may hold values from -2 to 2
Outputs:
- mesh_out: bfloat16 [81920, 512], P('patch', 'hidden')
- edge_out: bfloat16 [131072, 512], P('patch', 'hidden')
Inputs may be any that keep to these rules, and one draw needn't show every extreme that they name: `mesh_slot`: A permutation of the mesh node ids 0 to 81919; owner block p holds mesh rows p * 5120 to (p + 1) * 5120 - 1. `senders`: edge slots of block p (slots p * 8192 to (p + 1) * 8192 - 1) send from grid nodes p * 3072 to (p + 1) * 3072 - 1. Only the first edge_counts[p] slots of block p are live; some block is full.
All inputs are finite; a program needn't handle non-finite values.
Results may differ from a plain program's by a relative error of at most 0.014.
Values may be sent and summed in bfloat16 or wider, within the bound.
A program may use at most 192 MiB of HBM per device.

v0:
```python
import jax
import jax.numpy as jnp
from jax import lax
from jax.sharding import PartitionSpec as P

EPSILON = 1e-05


def as_sent(x):
    return jax.tree.map(lambda a: a.astype(jnp.bfloat16) if a.dtype == jnp.float32 else a, x)


def from_everyone(x, axis):
    copies = jnp.broadcast_to(x, (lax.axis_size(axis), *x.shape))
    return lax.all_to_all(copies, axis, split_axis=0, concat_axis=0, tiled=True)


def taken_together(x, axis):
    return from_everyone(x, axis).astype(jnp.float32).sum(axis=0)


def taken_together_2(x, axis):
    return from_everyone(x, axis).sum(axis=0)


def normalize(values, gain, offset, width, total_fn):
    totals = total_fn((jnp.sum(values, axis=1), jnp.sum(values * values, axis=1)))
    center = totals[0] / width
    spread = jnp.maximum(totals[1] / width - center * center, 0.0)
    centered = values - center[:, None]
    return centered * lax.rsqrt(spread + EPSILON)[:, None] * gain + offset


def edge_totals(values):
    return jax.tree.map(
        lambda part: part.astype(jnp.float32),
        jax.tree.map(lambda part: taken_together(part, "hidden"), as_sent(values)),
    )


def mesh_totals(values):
    return jax.tree.map(lambda part: taken_together_2(part, "hidden"), values)


def shards(
    grid_latent,
    mesh_latent,
    edge_latent,
    senders,
    receivers,
    mesh_slot,
    edge_counts,
    w_edge,
    w_sender,
    w_receiver,
    edge_bias,
    w_edge_out,
    edge_out_bias,
    edge_gain,
    edge_shift,
    w_mesh_in,
    w_message_in,
    mesh_bias,
    w_mesh_out,
    mesh_out_bias,
    mesh_gain,
    mesh_shift,
):
    patch_index = lax.axis_index("patch")
    column_index = lax.axis_index("hidden")
    own_grid = grid_latent.shape[0]
    own_edges = edge_latent.shape[0]
    slice_width = w_edge.shape[1]
    full_width = w_edge.shape[0]
    mesh_total = mesh_slot.shape[0]
    target_rows = jnp.take(mesh_slot, receivers)
    sender_local = senders - patch_index * own_grid
    live = (jnp.arange(own_edges, dtype=jnp.int32) < edge_counts[0]).astype(jnp.float32)
    receiver_part = jnp.dot(mesh_latent, w_receiver, preferred_element_type=jnp.float32).astype(
        jnp.bfloat16
    )
    table = lax.all_gather(receiver_part, "patch", axis=0, tiled=True)
    sender_part = jnp.dot(grid_latent, w_sender, preferred_element_type=jnp.float32)
    edge_pre = jnp.dot(edge_latent, w_edge, preferred_element_type=jnp.float32)
    edge_pre = (
        edge_pre
        + jnp.take(sender_part, sender_local, axis=0)
        + jnp.take(table, target_rows, axis=0).astype(jnp.float32)
        + edge_bias
    )
    edge_hidden = jax.nn.silu(edge_pre).astype(jnp.bfloat16)
    edge_partial = jnp.dot(edge_hidden, w_edge_out, preferred_element_type=jnp.float32)
    edge_summed = (
        lax.psum_scatter(
            edge_partial.astype(jnp.bfloat16), "hidden", scatter_dimension=1, tiled=True
        ).astype(jnp.float32)
        + edge_out_bias
    )
    message = normalize(edge_summed, edge_gain, edge_shift, full_width, edge_totals) * live[:, None]
    own_edge_cols = lax.dynamic_slice_in_dim(
        edge_latent, column_index * slice_width, slice_width, 1
    )
    edge_out = (own_edge_cols.astype(jnp.float32) + message).astype(jnp.bfloat16)
    spread_sums = jax.ops.segment_sum(message, target_rows, num_segments=mesh_total)
    received = lax.psum_scatter(
        spread_sums.astype(jnp.bfloat16), "patch", scatter_dimension=0, tiled=True
    )
    mesh_pre = jnp.dot(mesh_latent, w_mesh_in, preferred_element_type=jnp.float32) + mesh_bias
    gathered = lax.all_gather(received, "hidden", axis=1, tiled=True)
    mesh_pre = mesh_pre + jnp.dot(gathered, w_message_in, preferred_element_type=jnp.float32)
    mesh_hidden = jax.nn.silu(mesh_pre).astype(jnp.bfloat16)
    mesh_partial = jnp.dot(mesh_hidden, w_mesh_out, preferred_element_type=jnp.float32)
    mesh_summed = (
        lax.psum_scatter(
            mesh_partial.astype(jnp.bfloat16), "hidden", scatter_dimension=1, tiled=True
        ).astype(jnp.float32)
        + mesh_out_bias
    )
    mesh_update = normalize(mesh_summed, mesh_gain, mesh_shift, full_width, mesh_totals)
    own_mesh_cols = lax.dynamic_slice_in_dim(
        mesh_latent, column_index * slice_width, slice_width, 1
    )
    mesh_out = (own_mesh_cols.astype(jnp.float32) + mesh_update).astype(jnp.bfloat16)
    return (mesh_out, edge_out)


def solution(mesh):
    return jax.shard_map(
        shards,
        mesh=mesh,
        in_specs=(
            P("patch", None),
            P("patch", None),
            P("patch", None),
            P("patch"),
            P("patch"),
            P(),
            P("patch"),
            P(None, "hidden"),
            P(None, "hidden"),
            P(None, "hidden"),
            P("hidden"),
            P("hidden", None),
            P("hidden"),
            P("hidden"),
            P("hidden"),
            P(None, "hidden"),
            P(None, "hidden"),
            P("hidden"),
            P("hidden", None),
            P("hidden"),
            P("hidden"),
            P("hidden"),
        ),
        out_specs=(P("patch", "hidden"), P("patch", "hidden")),
        check_vma=False,
    )
```

profile of v0, /device:TPU:1, one launch (start us, length us, event | category | flops | bytes accessed | tf_op | source)
XLA Modules:
  0.0 574.4 jit_solution(239564840240605962)
XLA Ops:
  7.2 5.2 convolution_convert_fusion.2
  14.7 29.2 %gather_fusion.1 = f32[8192,64]{1,0:T(8,128)} fusion(f32[3072,64]{1,0:T(8,128)} %fusion.22, s32[8192]{0:T(1024)S(1)} %fusion.17), kind=kCustom, calls=%fused_computation.1 | custom fusion | bytes 4227072 | tf_op jit(solution)/shard_map/jit(_take)/gather | solution.py:87
  43.9 3.8 copy.67
  47.8 45.5 %gather_fusion = s32[8192]{0:T(1024)S(1)} fusion(s32[81920]{0:T(1024)S(1)} %copy-done.2, s32[8192]{0:T(1024)S(1)} %fusion.15), kind=kCustom, calls=%fused_computation | custom fusion | bytes 98304 | tf_op jit(solution)/shard_map/jit(_take)/gather | solution.py:76
  93.4 2.6 all-gather.3.cloned.1.call-done
  96.1 19.1 %copy.68 = bf16[81920,64]{1,0:T(8,128)(2,1)} copy(bf16[81920,64]{0,1:T(8,128)(2,1)} %all-gather.3.cloned.1.call-done) | data formatting | bytes 20971520 | tf_op jit(solution)/shard_map/all_gather | solution.py:82
  115.2 31.6 %gather_fusion.2 = bf16[8192,64]{1,0:T(8,128)(2,1)S(1)} fusion(bf16[81920,64]{1,0:T(8,128)(2,1)} %copy.68, s32[8192]{0:T(1024)S(1)} %fusion.16), kind=kCustom, calls=%fused_computation.2 | custom fusion | bytes 2129920 | tf_op jit(solution)/shard_map/jit(_take)/gather | solution.py:88
  147.7 13.5 %convolution_convert_fusion = bf16[8192,512]{0,1:T(8,128)(2,1)} fusion(bf16[64,512]{1,0:T(8,128)(2,1)S(1)} %copy-done.16, bf16[8192,512]{1,0:T(8,128)(2,1)} %param.24, bf16[512,64]{0,1:T(8,128)(2,1)S(1)} %copy-done.17, f32[8192,64]{0,1:T(8,128)} %copy.67, f32[64]{0:T(128)S(1)} %copy-done.18, bf16[8192,64]{0,1:T(8,128)(2,1)S(1)} %copy.69, ...), kind=kOutput, calls=%fused_computation.6 | convolution fusion | flops 1083703296 | bytes 20070656 | tf_op jit(solution)/shard_map/dot_general | solution.py:92
  161.1 52.6 %reduce-scatter.4.cloned.1.call-done = bf16[8192,64]{0,1:T(8,128)(2,1)} async-done(((bf16[8192,512]{0,1:T(8,128)(2,1)}), bf16[8192,64]{0,1:T(8,128)(2,1)}) %reduce-scatter.4.cloned.1.call-update) | async-done | bytes 1048592 | tf_op jit(solution)/shard_map/reduce_scatter | solution.py:94
  218.3 4.5 all-to-all-start.1
  228.8 4.8 all-to-all-start
  234.0 4.9 all-to-all-done
  239.3 2.9 add_convert_fusion
  242.2 2.7 copy.72
  244.9 60.8 %scatter_custom_fusion = f32[81920,64]{1,0:T(8,128)} fusion(s32[8192]{0:T(1024)S(1)} %get-tuple-element.7, f32[8192,64]{1,0:T(8,128)} %copy.72, f32[]{:T(128)} %constant.43.clone.1), kind=kCustom, calls=%fused_computation.4 | custom fusion | flops 524288 | bytes 20972032 | tf_op jit(solution)/shard_map/scatter-add | solution.py:104
  305.6 21.2 %convert_element_type.71 = bf16[81920,64]{1,0:T(8,128)(2,1)} convert(f32[81920,64]{1,0:T(8,128)} %scatter_custom_fusion) | non-fusion elementwise | flops 5242880 | bytes 31457280 | tf_op jit(solution)/shard_map/convert_element_type | solution.py:106
  327.2 131.3 %reduce-scatter.6.cloned.1.call-done = bf16[5120,64]{1,0:T(8,128)(2,1)} async-done(((bf16[81920,64]{1,0:T(8,128)(2,1)}), bf16[5120,64]{1,0:T(8,128)(2,1)}) %reduce-scatter.6.cloned.1.call-update) | async-done | bytes 655376 | tf_op jit(solution)/shard_map/reduce_scatter | solution.py:105
  460.9 4.2 convolution_add_fusion.2
  465.1 32.3 %all-gather.5.cloned.1.call-done = bf16[5120,512]{0,1:T(8,128)(2,1)} async-done(((bf16[5120,64]{0,1:T(8,128)(2,1)}), bf16[5120,512]{0,1:T(8,128)(2,1)}) %all-gather.5.cloned.1.call-update) | async-done | bytes 5242896 | tf_op jit(solution)/shard_map/all_gather | solution.py:109
  497.4 7.2 %convolution_convert_fusion.1 = bf16[5120,512]{0,1:T(8,128)(2,1)} fusion(bf16[64,512]{1,0:T(8,128)(2,1)S(1)} %copy-done.7, f32[5120,64]{0,1:T(8,128)S(1)} %convolution_add_fusion.2, bf16[512,64]{0,1:T(8,128)(2,1)S(1)} %copy-done.8, bf16[5120,512]{0,1:T(8,128)(2,1)} %all-gather.5.cloned.1.call-done), kind=kOutput, calls=%fused_computation.10 | convolution fusion | flops 675676160 | bytes 11927552 | tf_op jit(solution)/shard_map/dot_general | solution.py:112
  504.7 37.2 %reduce-scatter.8.cloned.1.call-done = bf16[5120,64]{0,1:T(8,128)(2,1)} async-done(((bf16[5120,512]{0,1:T(8,128)(2,1)}), bf16[5120,64]{0,1:T(8,128)(2,1)}) %reduce-scatter.8.cloned.1.call-update) | async-done | bytes 655376 | tf_op jit(solution)/shard_map/reduce_scatter | solution.py:114
  543.4 11.2 %all_to_all.24 = f32[8,1,5120]{2,1,0:T(1,128)S(1)} all-to-all(f32[8,1,5120]{2,1,0:T(1,128)S(1)} %broadcast_in_dim.69), channel_id=1, replica_groups=mesh['patch'=16,'hidden'=8] {'hidden'}, dimensions={0} | all-to-all | bytes 327680 | tf_op jit(solution)/shard_map/all_to_all | solution.py:15
  555.4 4.2 all-to-all-start.3
  559.6 3.0 constant_dynamic-slice_fusion.1
  (82 shorter events, 24.0 us)
Async XLA Ops:
  7.2 5.4 copy-start
  7.2 5.3 copy-start.3
  7.2 5.3 copy-start.5
  7.2 88.9 %all-gather.3.cloned.1.call-start = ((), (), s32[]{:S(2)}) async-start(), calls=%async_computation.7 | async-start | bytes 11141120 | tf_op jit(solution)/shard_map/all_gather | solution.py:82
  12.4 201.3 %reduce-scatter.4.cloned.1.call-start = ((), (), s32[]{:S(2)}) async-start(), calls=%async_computation.8 | async-start | bytes 9437184 | tf_op jit(solution)/shard_map/reduce_scatter | solution.py:94
  43.9 3.8 copy-start.4
  43.9 3.8 copy-start.2
  161.1 52.7 %copy-start.9 = (f32[64]{0:T(128)S(1)}, f32[64]{0:T(128)}, u32[]{:S(2)}) copy-start(f32[64]{0:T(128)} %param.34) | copy-start | bytes 772
  218.3 10.5 %all-to-all-start.1 = ((bf16[8,2,4096]{2,1,0:T(2,128)(2,1)}), bf16[8,2,4096]{2,1,0:T(2,128)(2,1)S(1)}, u32[]{:S(2)}, u32[]{:S(2)}) async-start(bf16[8,2,4096]{2,1,0:T(2,128)(2,1)} %reshape.119), calls=%async_computation.2 | async-start | bytes 262144 | tf_op jit(solution)/shard_map/all_to_all | solution.py:15
  225.9 13.4 %copy-start.12 = (f32[64]{0:T(128)S(1)}, f32[64]{0:T(128)}, u32[]{:S(2)}) copy-start(f32[64]{0:T(128)} %param.36) | copy-start | bytes 772
  225.9 13.4 %copy-start.13 = (f32[64]{0:T(128)S(1)}, f32[64]{0:T(128)}, u32[]{:S(2)}) copy-start(f32[64]{0:T(128)} %param.35) | copy-start | bytes 772
  228.8 10.1 %all-to-all-start = ((bf16[8,2,4096]{2,1,0:T(2,128)(2,1)}), bf16[8,2,4096]{2,1,0:T(2,128)(2,1)S(1)}, u32[]{:S(2)}, u32[]{:S(2)}) async-start(bf16[8,2,4096]{2,1,0:T(2,128)(2,1)} %reshape.121), calls=%async_computation.1 | async-start | bytes 262144 | tf_op jit(solution)/shard_map/all_to_all | solution.py:15
  233.6 224.9 %reduce-scatter.6.cloned.1.call-start = ((), (), s32[]{:S(2)}) async-start(), calls=%async_computation.9 | async-start | bytes 22282240 | tf_op jit(solution)/shard_map/reduce_scatter | solution.py:105
  326.9 134.0 %copy-start.6 = (bf16[512,64]{0,1:T(8,128)(2,1)S(1)}, bf16[512,64]{0,1:T(8,128)(2,1)}, u32[]{:S(2)}) copy-start(bf16[512,64]{0,1:T(8,128)(2,1)} %param.37) | copy-start | bytes 196612
  326.9 134.0 %copy-start.10 = (f32[64]{0:T(128)S(1)}, f32[64]{0:T(128)}, u32[]{:S(2)}) copy-start(f32[64]{0:T(128)} %param.39) | copy-start | bytes 772
  326.9 170.5 %all-gather.5.cloned.1.call-start = ((), (), s32[]{:S(2)}) async-start(), calls=%async_computation.10 | async-start | bytes 5898240 | tf_op jit(solution)/shard_map/all_gather | solution.py:109
  460.8 36.6 %copy-start.7 = (bf16[64,512]{1,0:T(8,128)(2,1)S(1)}, bf16[64,512]{1,0:T(8,128)(2,1)}, u32[]{:S(2)}) copy-start(bf16[64,512]{1,0:T(8,128)(2,1)} %param.40) | copy-start | bytes 196612
  460.8 36.6 %copy-start.8 = (bf16[512,64]{0,1:T(8,128)(2,1)S(1)}, bf16[512,64]{0,1:T(8,128)(2,1)}, u32[]{:S(2)}) copy-start(bf16[512,64]{0,1:T(8,128)(2,1)} %param.38) | copy-start | bytes 196612
  460.8 81.0 %reduce-scatter.8.cloned.1.call-start = ((), (), s32[]{:S(2)}) async-start(), calls=%async_computation.11 | async-start | bytes 5898240 | tf_op jit(solution)/shard_map/reduce_scatter | solution.py:114
  504.6 37.2 %copy-start.11 = (f32[64]{0:T(128)S(1)}, f32[64]{0:T(128)}, u32[]{:S(2)}) copy-start(f32[64]{0:T(128)} %param.41) | copy-start | bytes 772
  555.4 9.8 %all-to-all-start.3 = ((f32[8,1,5120]{2,1,0:T(1,128)}), f32[8,1,5120]{2,1,0:T(1,128)S(1)}, u32[]{:S(2)}, u32[]{:S(2)}) async-start(f32[8,1,5120]{2,1,0:T(1,128)} %broadcast_in_dim.70), calls=%async_computation.6 | async-start | bytes 327680 | tf_op jit(solution)/shard_map/all_to_all | solution.py:15
  559.6 5.7 copy-start.14
  559.6 5.7 copy-start.15
  559.6 8.3 %copy-start.1 = (bf16[3072,512]{1,0:T(8,128)(2,1)S(1)}, bf16[3072,512]{1,0:T(8,128)(2,1)}, u32[]{:S(2)}) copy-start(bf16[3072,512]{1,0:T(8,128)(2,1)} %param.22) | copy-start | bytes 9437188
  (3 other events, 2.6 us)
Sparse Core Ops, SparseCore 0:
  12.6 83.4 all-gather.2
  161.3 52.4 reduce-scatter.3
  327.0 131.4 reduce-scatter.5
  460.9 36.4 all-gather.4
  504.8 37.0 reduce-scatter.7
where the time goes:
time: 576 us; the launch traced here: 574 us
  waiting for transfers between devices  261 us (45%)
  local copies, waits for them, and re-layouts  147 us (26%)
  other arithmetic  94.2 us (16%)
  matrix products  32.2 us (6%)
  between operations  14.8 us (3%)
  starting transfers between devices  13.9 us (2%)
  blocking collectives  11.2 us (2%)
    reduce_scatter x1, waiting for transfers between devices, shards(): lax.psum_scatter(spread_sums.astype(jnp.bfloat16), 'patch', scatter_dimen...  131 us
    scatter-add x1, other arithmetic, shards(): jax.ops.segment_sum(message, target_rows, num_segments=mesh_total)  60.8 us
    reduce_scatter x1, waiting for transfers between devices, shards(): lax.psum_scatter(edge_partial.astype(jnp.bfloat16), 'hidden', scatter_dim...  52.6 us
    gather x1, local copies, waits for them, and re-layouts, shards(): target_rows = jnp.take(mesh_slot, receivers)  45.5 us
    reduce_scatter x1, waiting for transfers between devices, shards(): lax.psum_scatter(mesh_partial.astype(jnp.bfloat16), 'hidden', scatter_dim...  37.2 us
    gather x2, local copies, waits for them, and re-layouts, shards(): jnp.take(sender_part, sender_local, axis=0)  33.1 us
    gather x2, local copies, waits for them, and re-layouts, shards(): jnp.take(table, target_rows, axis=0).astype(jnp.float32)  32.4 us
    all_gather x1, waiting for transfers between devices, shards(): gathered = lax.all_gather(received, 'hidden', axis=1, tiled=True)  32.3 us
  transfers between devices with their start and end apart: 8, of which 7 were waited for; matrix products, arithmetic and copies ran while one was open for 17% of the time, Pallas kernels for 0%

commit v1 on v0

v1 whole, which is shorter than its diff:
```python
import jax
import jax.numpy as jnp
from jax import lax
from jax.experimental import pallas as pl
from jax.experimental.pallas import tpu as pltpu
from jax.sharding import PartitionSpec as P

EPSILON = 1e-05
F32 = jnp.float32
BF16 = jnp.bfloat16
NP = 16
NH = 8
LAT = 512
GRID = 3072
EDGE = 8192
MESH = 5120
SUB = MESH // NH
BLK = EDGE // NH
LW = LAT // NH
TAB = NP * MESH // 128
C_OWN, C_NEAR, C_FAR = 384, 224, 64
C_BLK = 176
NROW = C_OWN + 2 * C_NEAR + 13 * C_FAR
NCOMP = NH * C_BLK
MCH = 208
DEV = pl.DeviceIdType.MESH


def base_of(s):
    if s == 1:
        return 0
    if s == 15:
        return C_NEAR
    if s == 0:
        return 2 * C_NEAR + 13 * C_FAR
    return 2 * C_NEAR + C_FAR * (s - 2)


def cap_of(s):
    return C_OWN if s == 0 else (C_NEAR if s in (1, 15) else C_FAR)


def iota(shape, dim):
    return lax.broadcasted_iota(jnp.int32, shape, dim).astype(F32)


def dot_nn(a, b):
    return lax.dot_general(a, b, (((1,), (0,)), ((), ())), preferred_element_type=F32)


def dot_nt(a, b):
    return lax.dot_general(a, b, (((1,), (1,)), ((), ())), preferred_element_type=F32)


def onehot(mask):
    return jnp.where(mask, 1.0, 0.0).astype(BF16)


def col_of(row):
    eye = iota((128, 128), 0) == iota((128, 128), 1)
    return jnp.sum(jnp.where(eye, row, 0.0), axis=1, keepdims=True)


def row_of(col):
    eye = iota((128, 128), 0) == iota((128, 128), 1)
    return jnp.sum(jnp.where(eye, col, 0.0), axis=0, keepdims=True)


def norm_rows(values, gain, offset):
    center = jnp.sum(values, axis=1, keepdims=True) * (1.0 / LAT)
    centered = values - center
    spread = jnp.sum(centered * centered, axis=1, keepdims=True) * (1.0 / LAT)
    return centered * lax.rsqrt(spread + EPSILON) * gain + offset


def silu(v):
    return v / (1.0 + jnp.exp(-v))


def kernel(
    recv_i, send_i, slot, cnt, el_hbm, grid_hbm, mesh_hbm,
    w0, w1, w2, w3, w4, w5, w6,
    b0, b1, b2, b3, b4, b5, b6, b7,
    mo_hbm, eo_hbm, flag_ref,
    el, grid, blk, wfull, tb, tbr, oh, s_ref, sub_ref, r_ref, sd_ref, m_ref, rk_ref, o_ref,
    posb, posc, aq, bq, req_acc, req, reqr, mb, m2_ref, posx,
    xcm, metac, xb, pre, srow, soh, serve, recvrows, scoh, msgb, mrecv, eob, pcrow, eoc, recvx,
    mot, eot, summed, vecs, flagr,
    lsem, wlsem, t_ss, t_rs, w_ss, w_rs, f_ss, f_rs, q_ss, q_rs, g_ss, g_rs, m_ss, m_rs,
    x_ss, x_rs, mo_ss, mo_rs, eo_ss, eo_rs, fl_ss, fl_rs,
):
    p = lax.axis_index("patch")
    h = lax.axis_index("hidden")
    hf = h.astype(F32)
    pf = p.astype(F32)

    def hp(d):
        return lax.rem(h + d, NH)

    def pp(s):
        return lax.rem(p + s, NP)

    def remote(src, dst, ss, rs, dev):
        return pltpu.make_async_remote_copy(
            src_ref=src, dst_ref=dst, send_sem=ss, recv_sem=rs, device_id=dev, device_id_type=DEV
        )

    loads = [
        pltpu.make_async_copy(
            mesh_hbm.at[pl.ds(pl.multiple_of(h * SUB, SUB), SUB), :], blk, lsem.at[2]
        ),
        pltpu.make_async_copy(el_hbm, el, lsem.at[0]),
        pltpu.make_async_copy(grid_hbm, grid, lsem.at[1]),
    ]
    wsrc = (w0, w1, w2, w3, w4, w5, w6)
    wl = [pltpu.make_async_copy(wsrc[k], wfull.at[h, k], wlsem.at[k]) for k in range(7)]
    for c in wl:
        c.start()
    for c in loads:
        c.start()
    barrier = pltpu.get_barrier_semaphore()
    for d in range(1, NH):
        pl.semaphore_signal(barrier, inc=1, device_id=(p, hp(d)), device_id_type=DEV)
    for s in range(1, NP):
        pl.semaphore_signal(barrier, inc=1, device_id=(pp(s), h), device_id_type=DEV)

    h8 = pl.multiple_of(h * 8, 8)
    rr = recv_i[pl.ds(h8, 8), :]
    rhi = lax.shift_right_logical(rr, 7).astype(F32)
    rlo = (rr & 127).astype(F32)
    vt = slot[...].astype(F32).T
    va = jnp.floor(vt * (1.0 / 256.0))
    vb = vt - va * 256.0
    i640 = iota((TAB, 128), 0)
    for k in range(8):
        oh[:, 128 * k : 128 * (k + 1)] = onehot(i640 == rhi[k : k + 1, :])
    ohv = oh[...]
    la = dot_nn((va - 256.0).astype(BF16), ohv)
    lb = dot_nn(vb.astype(BF16), ohv)
    i128 = iota((128, 128), 0)
    for k in range(8):
        pick = i128 == rlo[k : k + 1, :]
        both = (la[:, 128 * k : 128 * (k + 1)] + 256.0) * 256.0 + lb[:, 128 * k : 128 * (k + 1)]
        tb[k : k + 1, :] = jnp.sum(jnp.where(pick, both, 0.0), axis=0, keepdims=True)
    for k, b in enumerate((b0, b1, b2, b3, b4, b5, b6, b7)):
        tb[8 + k : 9 + k, 0:LW] = b[...]
        tb[8 + k : 9 + k, LW:128] = b[...]

    pl.semaphore_wait(barrier, NH - 1 + NP - 1)
    t_copies = [
        remote(tb, tbr.at[h], t_ss.at[d], t_rs.at[d], (p, hp(d))) for d in range(1, NH)
    ]
    for c in t_copies:
        c.start()
    tbr[h] = tb[...]
    for c in wl:
        c.wait()
    partner = h + 1 - 2 * lax.rem(h, 2)
    w_copies = []
    for part, (lo, n) in enumerate(((0, 4), (4, 3))):
        for d in (1, 3, 2):
            i = part * 4 + d
            c = remote(
                wfull.at[h, pl.ds(lo, n)], wfull.at[h, pl.ds(lo, n)], w_ss.at[i], w_rs.at[i],
                (p, hp(2 * d)),
            )
            c.start()
            w_copies.append(c)
        c = remote(
            wfull.at[h, pl.ds(lo, n)], wfull.at[h, pl.ds(lo, n)], f_ss.at[part * 4], f_rs.at[part * 4],
            (p, partner),
        )
        c.start()
        w_copies.append(c)

    def from_chip(part, d):
        lo, n = ((0, 4), (4, 3))[part]
        src_h = lax.rem(h + NH - 2 * d, NH)
        ref = wfull.at[src_h, pl.ds(lo, n)]
        i = part * 4 + d
        return (
            remote(ref, ref, w_ss.at[i], w_rs.at[i], (p, hp(2 * d))),
            remote(ref, ref, f_ss.at[i], f_rs.at[i], (p, partner)),
        )

    def forward(part):
        for d in (1, 3, 2):
            arrival, fwd = from_chip(part, d)
            arrival.wait_recv()
            fwd.start()

    def weights_ready(part):
        lo, n = ((0, 4), (4, 3))[part]
        for d in range(4):
            src_h = lax.rem(partner + NH - 2 * d, NH)
            ref = wfull.at[src_h, pl.ds(lo, n)]
            remote(ref, ref, f_ss.at[part * 4 + d], f_rs.at[part * 4 + d], (p, partner)).wait_recv()

    tri = jnp.where(iota((128, 256), 1) < 128.0,
                    jnp.where(iota((128, 256), 0) < iota((128, 256), 1), 1.0, 0.0), 1.0).astype(BF16)
    i16 = iota((16, 128), 0)
    base16 = jnp.where(
        i16 == 0.0, float(base_of(0)),
        jnp.where(i16 == 1.0, 0.0, jnp.where(i16 == 15.0, float(C_NEAR), 2.0 * C_NEAR + C_FAR * (i16 - 2.0))),
    )
    cap16 = jnp.where(i16 == 0.0, float(C_OWN), jnp.where((i16 == 1.0) | (i16 == 15.0), float(C_NEAR), float(C_FAR)))
    i48 = iota((48, 128), 0)

    for c in t_copies:
        c.wait_recv()

    tf = tbr[:, 0:8, :].reshape(64, 128)
    q = jnp.floor((tf + 0.5) * (1.0 / MESH))
    rem = tf - q * MESH
    sub = jnp.floor((rem + 0.5) * (1.0 / SUB))
    r1 = rem - sub * SUB + 1.0
    shift = q - pf
    shift = jnp.where(shift < 0.0, shift + NP, shift)
    eidx = lax.broadcasted_iota(jnp.int32, (64, 128), 0) * 128 + lax.broadcasted_iota(jnp.int32, (64, 128), 1)
    live = eidx < cnt[0]
    own = live & (sub == hf)
    s_ref[...] = jnp.where(own, shift, -1.0)
    sub_ref[...] = jnp.where(live, sub, -1.0)
    r_ref[...] = r1
    sd_ref[...] = (send_i[...] - p * GRID).astype(F32)
    o_ref[...] = dot_nn(onehot(own), tri)

    def mark(b, _):
        st = s_ref[pl.ds(pl.multiple_of(b * 8, 8), 8), :]
        for k in range(8):
            m_ref[pl.ds(pl.multiple_of(b * 128 + 16 * k, 16), 16), :] = onehot(i16 == st[k : k + 1, :])
        return 0

    lax.fori_loop(0, 8, mark, 0)
    rk_ref[...] = dot_nn(m_ref[...], tri)
    req_acc[...] = jnp.zeros_like(req_acc)

    def place(b, carry):
        counts, most = carry
        b8 = pl.ds(pl.multiple_of(b * 8, 8), 8)
        st = s_ref[b8, :]
        rt = r_ref[b8, :]
        ot = o_ref[b8, :]
        rowcount = jnp.zeros((1, 128), F32)
        pbs, pcs = [], []
        vhi = jnp.floor(rt * (1.0 / 256.0))
        vlo = rt - vhi * 256.0
        for k in range(8):
            i0 = pl.ds(pl.multiple_of(b * 128 + 16 * k, 16), 16)
            rk = rk_ref[i0, :]
            mk = m_ref[i0, :].astype(F32)
            rank = rk[:, :128] + counts
            counts = counts + rk[:, 128:]
            isown = st[k : k + 1, :] >= 0.0
            pb = jnp.sum(mk * (base16 + rank), axis=0, keepdims=True)
            rk1 = jnp.sum(mk * rank, axis=0, keepdims=True)
            pbs.append(jnp.where(isown, pb, -1.0))
            pcs.append(jnp.where(isown, ot[k : k + 1, :128] + rowcount, -1.0))
            rowcount = rowcount + ot[k : k + 1, 128:]
            qhi0 = jnp.floor(rk1 * (1.0 / 128.0))
            qlo = rk1 - qhi0 * 128.0
            qhi = jnp.where(isown & (qhi0 < 3.0), st[k : k + 1, :] * 3.0 + qhi0, -1.0)
            hit = i48 == qhi
            lanes = slice(128 * k, 128 * (k + 1))
            aq[0:48, lanes] = jnp.where(hit, vhi[k : k + 1, :], 0.0).astype(BF16)
            aq[48:96, lanes] = jnp.where(hit, vlo[k : k + 1, :], 0.0).astype(BF16)
            bq[:, lanes] = onehot(i128 == qlo)
        for k in range(8):
            posb[pl.ds(b * 8 + k, 1), :] = pbs[k]
            posc[pl.ds(b * 8 + k, 1), :] = pcs[k]
        req_acc[...] += dot_nt(aq[...], bq[...])
        return counts, jnp.maximum(most, rowcount)

    counts, most = lax.fori_loop(0, 8, place, (jnp.zeros((16, 128), F32), jnp.zeros((1, 128), F32)))
    over = jnp.max(jnp.where(counts > cap16, 1.0, 0.0), axis=0, keepdims=True)
    over = jnp.maximum(over, jnp.where(most > float(C_BLK), 1.0, 0.0))
    for s in range(NP):
        req[s, 0:3, :] = req_acc[3 * s : 3 * s + 3, :] * 256.0 + req_acc[48 + 3 * s : 48 + 3 * s + 3, :] - 1.0
        req[s, 3:7, :] = jnp.full((4, 128), -1.0, F32)
        req[s, 7:8, :] = over
    q_copies = [
        remote(req.at[s], reqr.at[s], q_ss.at[s], q_rs.at[s], (pp(s), h)) for s in range(1, NP)
    ]
    for c in q_copies:
        c.start()
    reqr[0] = req[0]

    for c in loads:
        c.wait()
    ic = iota((C_BLK, 128), 0)
    mb[...] = jnp.zeros_like(mb)

    def compact(b, _):
        b8 = pl.ds(pl.multiple_of(b * 8, 8), 8)
        pct = posc[b8, :]
        pbt = posb[b8, :]
        sdt = sd_ref[b8, :]
        phi = jnp.floor(pbt * (1.0 / 128.0))
        plo = pbt - phi * 128.0
        shi = jnp.floor(sdt * (1.0 / 128.0))
        slo = sdt - shi * 128.0
        for k in range(8):
            lanes = slice(128 * k, 128 * (k + 1))
            oh[0:C_BLK, lanes] = onehot(ic == pct[k : k + 1, :])
            mb[0:1, lanes] = phi[k : k + 1, :].astype(BF16)
            mb[1:2, lanes] = plo[k : k + 1, :].astype(BF16)
            mb[2:3, lanes] = shi[k : k + 1, :].astype(BF16)
            mb[3:4, lanes] = slo[k : k + 1, :].astype(BF16)
            mb[4:5, lanes] = jnp.ones((1, 128), BF16)
        ohb = oh[0:C_BLK, :]
        rows = pl.ds(pl.multiple_of(b * C_BLK, 16), C_BLK)
        xcm[rows, 0:LAT] = dot_nn(ohb, el[pl.ds(pl.multiple_of(b * BLK, BLK), BLK), :]).astype(BF16)
        meta = dot_nt(ohb, mb[...])
        xcm[rows, LAT : LAT + 128] = meta.astype(BF16)
        metac[rows, :] = jnp.broadcast_to(
            meta[:, 0:1] * 128.0 + meta[:, 1:2] + (meta[:, 4:5] - 1.0), (C_BLK, 128)
        )
        return 0

    lax.fori_loop(0, 8, compact, 0)
    for k in range(NCOMP // 128):
        pcrow[:, 128 * k : 128 * (k + 1)] = jnp.broadcast_to(
            row_of(metac[128 * k : 128 * (k + 1), :]), (8, 128)
        )

    for c in q_copies:
        c.wait_recv()
    for s in range(NP):
        b, c = base_of(s), cap_of(s)
        for j in range(-(-c // 128)):
            n = min(128, c - 128 * j)
            srow[0:1, b + 128 * j : b + 128 * j + n] = reqr[s, j : j + 1, 0:n]
    flag_p = jnp.max(reqr[:, 7, :], axis=0, keepdims=True)
    flagr[h] = jnp.broadcast_to(flag_p, (8, 128))
    il640 = iota((128, SUB), 1)
    for k in range(NROW // 128):
        soh[128 * k : 128 * (k + 1), :] = onehot(il640 == col_of(srow[0:1, 128 * k : 128 * (k + 1)]))

    def serve_rows(c, _):
        rows = pl.ds(pl.multiple_of(c * 2 * MCH, 16), 2 * MCH)
        serve[rows, :] = dot_nn(soh[rows, :], blk[...]).astype(BF16)
        return 0

    lax.fori_loop(0, NROW // (2 * MCH), serve_rows, 0)
    order = (1, 15) + tuple(range(2, 15))
    g_copies = []
    for s in order:
        rows = pl.ds(base_of(s), cap_of(s))
        c = remote(
            serve.at[rows], recvrows.at[rows], g_ss.at[s], g_rs.at[s], (lax.rem(p + NP - s, NP), h)
        )
        c.start()
        g_copies.append(c)
    ownr = slice(base_of(0), base_of(0) + C_OWN)
    recvrows[ownr, :] = serve[ownr, :]
    fl_copies = [
        remote(flagr.at[h], flagr.at[h], fl_ss.at[d], fl_rs.at[d], (p, hp(d))) for d in range(1, NH)
    ]
    for c in fl_copies:
        c.start()
    isub = iota((SUB, 128), 0)
    for k in range(NROW // 128):
        scoh[:, 128 * k : 128 * (k + 1)] = onehot(isub == srow[0:1, 128 * k : 128 * (k + 1)])
    forward(0)

    def arrange(c, _):
        rows = pl.ds(pl.multiple_of(c * MCH, 16), MCH)
        j0 = (c * MCH).astype(F32)
        perm = onehot(iota((MCH, NCOMP), 0) + j0 == pcrow[0:1, :])
        x = dot_nn(perm, xcm[...])
        xb[rows, :] = x[:, 0:LAT].astype(BF16)
        pick = x[:, LAT + 2 : LAT + 3] * 128.0 + x[:, LAT + 3 : LAT + 4]
        pre[rows, :] = dot_nn(onehot(iota((MCH, GRID), 1) == pick), grid[...])
        return 0

    lax.fori_loop(0, NROW // MCH, arrange, 0)
    weights_ready(0)
    lane = lax.broadcasted_iota(jnp.int32, (8, 128), 1)
    for j in range(4):
        even, odd = tbr[2 * j, 8:16, :], tbr[2 * j + 1, 8:16, :]
        vecs[:, 128 * j : 128 * (j + 1)] = jnp.where(lane < LW, even, odd)

    def full(k):
        return wfull[:, k].reshape(LAT, LAT)

    def first(c, _):
        rows = pl.ds(pl.multiple_of(c * MCH, 16), MCH)
        pre[rows, :] = dot_nt(xb[rows, :], full(0)) + dot_nt(pre[rows, :].astype(BF16), full(1)) + vecs[0:1, :]
        return 0

    lax.fori_loop(0, NROW // MCH, first, 0)
    for c in g_copies:
        c.wait_recv()

    def mlp(c, _):
        rows = pl.ds(pl.multiple_of(c * MCH, 16), MCH)
        v = pre[rows, :] + dot_nt(recvrows[rows, :], full(2))
        hid = silu(v).astype(BF16)
        msg = norm_rows(dot_nn(hid, full(3)) + vecs[1:2, :], vecs[2:3, :], vecs[3:4, :])
        msgb[rows, :] = msg.astype(BF16)
        eob[rows, :] = (xb[rows, :].astype(F32) + msg).astype(BF16)
        return 0

    lax.fori_loop(0, NROW // MCH, mlp, 0)
    m_copies = []
    for s in order:
        rows = pl.ds(base_of(s), cap_of(s))
        c = remote(msgb.at[rows], mrecv.at[rows], m_ss.at[s], m_rs.at[s], (pp(s), h))
        c.start()
        m_copies.append(c)
    mrecv[ownr, :] = msgb[ownr, :]
    forward(1)

    def scatter_block(d, _):
        b = lax.rem(h + d, NH)
        rows = pl.ds(pl.multiple_of(b * C_BLK, 16), C_BLK)
        mine = pl.ds(pl.multiple_of(h * C_BLK, 16), C_BLK)
        perm = onehot(iota((C_BLK, NROW), 1) == metac[rows, 0:1])
        eoc[rows, :] = dot_nn(perm, eob[...]).astype(BF16)

        @pl.when(d > 0)
        def _():
            remote(eoc.at[rows], recvx.at[mine], x_ss.at[d], x_rs.at[d], (p, b)).start()

        @pl.when(d == 0)
        def _():
            recvx[mine, :] = eoc[rows, :]

        return 0

    lax.fori_loop(0, NH, scatter_block, 0)

    for c in m_copies:
        c.wait_recv()
    weights_ready(1)

    def sums(c, _):
        rows = pl.ds(pl.multiple_of(c * 128, 128), 128)
        summed[rows, :] = dot_nn(scoh[rows, :], mrecv[...]).astype(BF16)
        return 0

    lax.fori_loop(0, SUB // 128, sums, 0)

    def mesh(c, _):
        rows = pl.ds(pl.multiple_of(c * 128, 128), 128)
        x = blk[rows, :]
        v = dot_nt(x, full(4)) + dot_nt(summed[rows, :], full(5)) + vecs[4:5, :]
        hid = silu(v).astype(BF16)
        upd = norm_rows(dot_nn(hid, full(6)) + vecs[5:6, :], vecs[6:7, :], vecs[7:8, :])
        mot[:, rows] = (x.astype(F32) + upd).T.astype(BF16)
        return 0

    lax.fori_loop(0, SUB // 128, mesh, 0)
    mo_copies = []
    at_mesh = pl.ds(pl.multiple_of(h * SUB, 128), SUB)
    for d in range(1, NH):
        c = remote(
            mot.at[pl.ds(pl.multiple_of(hp(d) * LW, LW), LW), :], mo_hbm.at[:, at_mesh],
            mo_ss.at[d], mo_rs.at[d], (p, hp(d)),
        )
        c.start()
        mo_copies.append(c)
    mo_own = pltpu.make_async_copy(
        mot.at[pl.ds(pl.multiple_of(h * LW, LW), LW), :], mo_hbm.at[:, at_mesh], lsem.at[3]
    )
    mo_own.start()

    subt = sub_ref[pl.ds(h8, 8), :]
    i8 = iota((8, 128), 0)
    for k in range(8):
        m2_ref[8 * k : 8 * k + 8, :] = jnp.where(i8 == subt[k : k + 1, :], 1.0, 0.0)
    rk2 = dot_nn(m2_ref[...].astype(BF16), tri)
    seen = jnp.zeros((8, 128), F32)
    for k in range(8):
        rank = rk2[8 * k : 8 * k + 8, :128] + seen
        seen = seen + rk2[8 * k : 8 * k + 8, 128:]
        px = jnp.sum(m2_ref[8 * k : 8 * k + 8, :] * (i8 * float(C_BLK) + rank), axis=0, keepdims=True)
        posx[128 * k : 128 * (k + 1), :] = jnp.broadcast_to(
            col_of(jnp.where(subt[k : k + 1, :] >= 0.0, px, -1.0)), (128, 128)
        )
    for d in range(1, NH):
        src = pl.ds(pl.multiple_of(lax.rem(h + NH - d, NH) * C_BLK, 16), C_BLK)
        remote(recvx.at[src], recvx.at[src], x_ss.at[d], x_rs.at[d], (p, hp(d))).wait_recv()

    def edge_rows(c, _):
        slots = pl.ds(pl.multiple_of(c * 128, 128), 128)
        px = posx[slots, :]
        perm = onehot(iota((128, NCOMP), 1) == px[:, 0:1])
        moved = dot_nn(perm, recvx[...])
        at = pl.ds(pl.multiple_of(h * BLK + c * 128, 128), 128)
        out = jnp.where(px[:, 0:1] >= 0.0, moved, el[at, :].astype(F32))
        eot[:, slots] = out.T.astype(BF16)
        return 0

    lax.fori_loop(0, BLK // 128, edge_rows, 0)
    eo_copies = []
    at_edge = pl.ds(pl.multiple_of(h * BLK, 128), BLK)
    for d in range(1, NH):
        c = remote(
            eot.at[pl.ds(pl.multiple_of(hp(d) * LW, LW), LW), :], eo_hbm.at[:, at_edge],
            eo_ss.at[d], eo_rs.at[d], (p, hp(d)),
        )
        c.start()
        eo_copies.append(c)
    eo_own = pltpu.make_async_copy(
        eot.at[pl.ds(pl.multiple_of(h * LW, LW), LW), :], eo_hbm.at[:, at_edge], lsem.at[4]
    )
    eo_own.start()

    for d in range(1, NH):
        src = lax.rem(h + NH - d, NH)
        remote(flagr.at[src], flagr.at[src], fl_ss.at[d], fl_rs.at[d], (p, hp(d))).wait_recv()
    flag_ref[...] = jnp.max(flagr[...], axis=0)
    for c in t_copies + w_copies + q_copies + g_copies + fl_copies + m_copies:
        c.wait_send()
    for part in range(2):
        for d in (1, 3, 2):
            from_chip(part, d)[1].wait_send()
    for d in range(1, NH):
        rows = pl.ds(pl.multiple_of(hp(d) * C_BLK, 16), C_BLK)
        remote(eoc.at[rows], eoc.at[rows], x_ss.at[d], x_rs.at[d], (p, hp(d))).wait_send()
    for d in range(1, NH):
        src_h = lax.rem(h + NH - d, NH)
        at_m = pl.ds(pl.multiple_of(src_h * SUB, 128), SUB)
        at_e = pl.ds(pl.multiple_of(src_h * BLK, 128), BLK)
        remote(mo_hbm.at[:, at_m], mo_hbm.at[:, at_m], mo_ss.at[d], mo_rs.at[d], (p, hp(d))).wait_recv()
        remote(eo_hbm.at[:, at_e], eo_hbm.at[:, at_e], eo_ss.at[d], eo_rs.at[d], (p, hp(d))).wait_recv()
    for c in mo_copies + eo_copies:
        c.wait_send()
    mo_own.wait()
    eo_own.wait()


def sparse_step(grid_latent, mesh_latent, edge_latent, senders, receivers, mesh_slot, edge_counts,
                w_edge, w_sender, w_receiver, edge_bias, w_edge_out, edge_out_bias, edge_gain, edge_shift,
                w_mesh_in, w_message_in, mesh_bias, w_mesh_out, mesh_out_bias, mesh_gain, mesh_shift):
    V = pltpu.VMEM
    vm = pl.BlockSpec(memory_space=pltpu.VMEM)
    anyspec = pl.BlockSpec(memory_space=pl.ANY)
    weights = (w_edge.T, w_sender.T, w_receiver.T, w_edge_out, w_mesh_in.T, w_message_in.T, w_mesh_out)
    vectors = tuple(v.reshape(1, LW) for v in (
        edge_bias, edge_out_bias, edge_gain, edge_shift, mesh_bias, mesh_out_bias, mesh_gain, mesh_shift))
    dma = pltpu.SemaphoreType.DMA
    scratch = [
        V((EDGE, LAT), BF16), V((GRID, LAT), BF16), V((SUB, LAT), BF16), V((NH, 7, LW, LAT), BF16),
        V((16, 128), F32), V((NH, 16, 128), F32), V((TAB, 1024), BF16),
        V((64, 128), F32), V((64, 128), F32), V((64, 128), F32), V((64, 128), F32),
        V((1024, 128), BF16), V((1024, 256), F32), V((64, 256), F32),
        V((64, 128), F32), V((64, 128), F32), V((96, 1024), BF16), V((128, 1024), BF16),
        V((96, 128), F32), V((NP, 8, 128), F32), V((NP, 8, 128), F32), V((128, 1024), BF16),
        V((64, 128), F32), V((BLK, 128), F32),
        V((NCOMP, LAT + 128), BF16), V((NCOMP, 128), F32), V((NROW, LAT), BF16), V((NROW, LAT), F32),
        V((8, NROW), F32), V((NROW, SUB), BF16), V((NROW, LAT), BF16), V((NROW, LAT), BF16),
        V((SUB, NROW), BF16), V((NROW, LAT), BF16), V((NROW, LAT), BF16), V((NROW, LAT), BF16),
        V((8, NCOMP), F32), V((NCOMP, LAT), BF16), V((NCOMP, LAT), BF16),
        V((LAT, SUB), BF16), V((LAT, BLK), BF16), V((SUB, LAT), BF16), V((8, LAT), F32), V((NH, 8, 128), F32),
        dma((5,)), dma((7,)), dma((8,)), dma((8,)), dma((8,)), dma((8,)), dma((8,)), dma((8,)),
        dma((16,)), dma((16,)), dma((16,)), dma((16,)), dma((16,)), dma((16,)),
        dma((8,)), dma((8,)), dma((8,)), dma((8,)), dma((8,)), dma((8,)), dma((8,)), dma((8,)),
    ]
    mo_t, eo_t, flag = pl.pallas_call(
        kernel,
        out_shape=(
            jax.ShapeDtypeStruct((LW, MESH), BF16),
            jax.ShapeDtypeStruct((LW, EDGE), BF16),
            jax.ShapeDtypeStruct((8, 128), F32),
        ),
        in_specs=[vm, vm, vm, pl.BlockSpec(memory_space=pltpu.SMEM), anyspec, anyspec, anyspec]
        + [anyspec] * 7 + [vm] * 8,
        out_specs=(anyspec, anyspec, vm),
        scratch_shapes=scratch,
        compiler_params=pltpu.CompilerParams(
            collective_id=0, has_side_effects=True, vmem_limit_bytes=62 * 1024 * 1024
        ),
        name="encoder",
    )(receivers.reshape(64, 128), senders.reshape(64, 128), mesh_slot.reshape(TAB, 128), edge_counts,
      edge_latent, grid_latent, mesh_latent, *weights, *vectors)
    return mo_t, eo_t, flag


def from_everyone(x, axis):
    copies = jnp.broadcast_to(x, (lax.axis_size(axis), *x.shape))
    return lax.all_to_all(copies, axis, split_axis=0, concat_axis=0, tiled=True)


def total_of(x, axis):
    return from_everyone(x, axis).sum(axis=0)


def scatter_columns(x):
    parts = x.astype(BF16).reshape(x.shape[0], NH, LW).transpose(1, 0, 2)
    got = lax.all_to_all(parts, "hidden", split_axis=0, concat_axis=0, tiled=True)
    return got.astype(F32).sum(axis=0)


def normalize(values, gain, offset):
    center = total_of(jnp.sum(values, axis=1), "hidden") / LAT
    centered = values - center[:, None]
    spread = total_of(jnp.sum(centered * centered, axis=1), "hidden") / LAT
    return centered * lax.rsqrt(spread + EPSILON)[:, None] * gain + offset


def general_step(grid_latent, mesh_latent, edge_latent, senders, receivers, mesh_slot, edge_counts,
                 w_edge, w_sender, w_receiver, edge_bias, w_edge_out, edge_out_bias, edge_gain, edge_shift,
                 w_mesh_in, w_message_in, mesh_bias, w_mesh_out, mesh_out_bias, mesh_gain, mesh_shift):
    column = lax.axis_index("hidden")
    target = jnp.take(mesh_slot, receivers)
    sender = senders - lax.axis_index("patch") * GRID
    live = (jnp.arange(EDGE, dtype=jnp.int32) < edge_counts[0]).astype(F32)
    proj = jnp.dot(mesh_latent, w_receiver, preferred_element_type=F32).astype(BF16)
    table = from_everyone(proj, "patch").reshape(NP * MESH, LW)
    edge_pre = (
        jnp.dot(edge_latent, w_edge, preferred_element_type=F32)
        + jnp.dot(jnp.take(grid_latent, sender, axis=0), w_sender, preferred_element_type=F32)
        + jnp.take(table, target, axis=0).astype(F32)
        + edge_bias
    )
    hid = silu(edge_pre).astype(BF16)
    edge_sum = scatter_columns(jnp.dot(hid, w_edge_out, preferred_element_type=F32)) + edge_out_bias
    message = normalize(edge_sum, edge_gain, edge_shift) * live[:, None]
    cols = lax.dynamic_slice_in_dim(edge_latent, column * LW, LW, 1)
    edge_out = (cols.astype(F32) + message).astype(BF16)
    sums = jax.ops.segment_sum(message, target, num_segments=NP * MESH).astype(BF16)
    got = lax.all_to_all(sums.reshape(NP, MESH, LW), "patch", split_axis=0, concat_axis=0, tiled=True)
    own = got.astype(F32).sum(axis=0).astype(BF16)
    summed = from_everyone(own, "hidden").transpose(1, 0, 2).reshape(MESH, LAT)
    mesh_pre = (
        jnp.dot(mesh_latent, w_mesh_in, preferred_element_type=F32)
        + jnp.dot(summed, w_message_in, preferred_element_type=F32)
        + mesh_bias
    )
    hid = silu(mesh_pre).astype(BF16)
    mesh_sum = scatter_columns(jnp.dot(hid, w_mesh_out, preferred_element_type=F32)) + mesh_out_bias
    update = normalize(mesh_sum, mesh_gain, mesh_shift)
    cols = lax.dynamic_slice_in_dim(mesh_latent, column * LW, LW, 1)
    return (cols.astype(F32) + update).astype(BF16).T, edge_out.T


def step(*args):
    mo_t, eo_t, flag = sparse_step(*args)

    def again(state):
        mo, eo = general_step(*args)
        return jnp.zeros_like(state[0]), mo, eo

    mo_t, eo_t = lax.cond(flag[0, 0] > 0.5, lambda: general_step(*args), lambda: (mo_t, eo_t))
    return mo_t.T, eo_t.T


def solution(mesh):
    return jax.shard_map(
        step,
        mesh=mesh,
        in_specs=(
            P("patch", None), P("patch", None), P("patch", None), P("patch"), P("patch"), P(), P("patch"),
            P(None, "hidden"), P(None, "hidden"), P(None, "hidden"), P("hidden"), P("hidden", None),
            P("hidden"), P("hidden"), P("hidden"), P(None, "hidden"), P(None, "hidden"), P("hidden"),
            P("hidden", None), P("hidden"), P("hidden"), P("hidden"),
        ),
        out_specs=(P("patch", "hidden"), P("patch", "hidden")),
        check_vma=False,
    )
```

time: 576 us -> 104 us (0.18)
  waiting for transfers between devices: 261 us -> 0 us
  local copies, waits for them, and re-layouts: 147 us -> 3.01 us
  Pallas kernels: 0 us -> 98.2 us
  other arithmetic: 94.2 us -> 0 us
  matrix products: 32.2 us -> 0 us
  starting transfers between devices: 13.9 us -> 0 us
  between operations: 14.8 us -> 1.96 us
  blocking collectives: 11.2 us -> 0 us
    reduce_scatter x3 -> x0, waiting for transfers between devices: 221 us -> none  [the longest x1 131 us: shards(): lax.psum_scatter(spread_sums.astype(jnp.bfloat16), 'patch', scatter_dimen...]
    gather x5 -> x0, local copies, waits for them, and re-layouts: 111 us -> none  [the longest x1 45.5 us: shards(): target_rows = jnp.take(mesh_slot, receivers)]
    pallas_call x0 -> x1, Pallas kernels: none -> 98.2 us  [sparse_step(): pl.pallas_call(kernel, out_shape=(jax.ShapeDtypeStruct((LW, MESH), BF16),...]
    scatter-add x1 -> x0, other arithmetic: 60.8 us -> none  [shards(): jax.ops.segment_sum(message, target_rows, num_segments=mesh_total)]
    all_gather x2 -> x0, waiting for transfers between devices: 35 us -> none  [the longest x1 32.3 us: shards(): gathered = lax.all_gather(received, 'hidden', axis=1, tiled=True)]
    dot_general x5 -> x0, matrix products: 32.2 us -> none  [the longest x1 13.5 us: shards(): jnp.dot(edge_hidden, w_edge_out, preferred_element_type=jnp.float32)]
    convert_element_type x4 -> x0, other arithmetic: 26.7 us -> none  [the longest x1 21.2 us: shards(): spread_sums.astype(jnp.bfloat16)]
    all_gather x1 -> x0, local copies, waits for them, and re-layouts: 19.1 us -> none  [shards(): table = lax.all_gather(receiver_part, 'patch', axis=0, tiled=True)]
  transfers between devices with their start and end apart: 8 -> 0, of which waited for: 7 -> 0; matrix products, arithmetic and copies ran while one was open for 17% -> 0% of each run, Pallas kernels for 0% -> 0%
where the time goes in v1:
time: 104 us; the launch traced here: 103 us
  Pallas kernels  98.2 us (94%)
  local copies, waits for them, and re-layouts  3.01 us (3%)
  between operations  1.96 us (2%)
    pallas_call x1, Pallas kernels, sparse_step(): pl.pallas_call(kernel, out_shape=(jax.ShapeDtypeStruct((LW, MESH), BF16),...  98.2 us

profile of v1, /device:TPU:1, one launch (start us, length us, event | category | flops | bytes accessed | tf_op | source)
XLA Modules:
  0.0 103.4 jit_solution(8903580960268196765)
XLA Ops:
  1.3 0.0 copy-start
  1.3 98.2 %encoder.1 = (bf16[64,5120]{1,0:T(8,128)(2,1)S(1)}, bf16[64,8192]{1,0:T(8,128)(2,1)S(1)}, f32[8,128]{1,0:T(8,128)}) custom-call(s32[64,128]{1,0:T(8,128)} %bitcast.57, s32[64,128]{1,0:T(8,128)} %bitcast.58, s32[640,128]{1,0:T(8,128)} %bitcast.49, s32[1]{0:T(128)S(6)} %copy.142.cnt, bf16[8192,512]{1,0:T(8,128)(2,1)} %el_hbm.1, bf16[3072,512]{1,0:T(8,128)(2,1)} %grid_hbm.1, ...), custom_call_target="tpu_custom_call" | custom-call | tf_op jit(solution)/shard_map/encoder/pallas_call | solution.py:561
  99.5 1.2 %slice.3 = f32[1,1]{1,0:T(1,128)} slice(f32[8,128]{1,0:T(8,128)} %get-tuple-element.77), slice={[0:1], [0:1]} | slice | bytes 8 | tf_op jit(solution)/shard_map/slice | solution.py:646
  101.4 0.0 copy-done
  101.4 0.2 conditional.1
  101.6 0.8 copy.143
  102.4 1.0 copy.144
Async XLA Ops:
  1.3 100.1 %copy-start = (s32[81920]{0:T(1024)S(1)}, s32[81920]{0:T(1024)}, u32[]{:S(2)}) copy-start(s32[81920]{0:T(1024)} %param.29) | copy-start | bytes 983044

commit v2 on v1

v2 whole, which is shorter than its diff:
```python
import jax
import jax.numpy as jnp
from jax import lax
from jax.experimental import pallas as pl
from jax.experimental.pallas import tpu as pltpu
from jax.sharding import PartitionSpec as P

EPSILON = 1e-05
F32 = jnp.float32
BF16 = jnp.bfloat16
NP = 16
NH = 8
LAT = 512
GRID = 3072
EDGE = 8192
MESH = 5120
SUB = MESH // NH
BLK = EDGE // NH
LW = LAT // NH
TAB = NP * MESH // 128
C_OWN, C_NEAR, C_FAR = 384, 224, 64
C_BLK = 176
NROW = C_OWN + 2 * C_NEAR + 13 * C_FAR
NCOMP = NH * C_BLK
MCH = 208
SCH = 352
EARLY = 8
FCH = 704
PCH = 416
UCH = 512
HALF = NCOMP // 2
DEV = pl.DeviceIdType.MESH
GROUPS = ((5, 6, 7, 8, 9, 10, 11), (2, 3, 4, 12, 13, 14), (1, 15))


def base_of(s):
    if s == 0:
        return NROW - C_OWN
    if s in (1, 15):
        return 13 * C_FAR + (C_NEAR if s == 15 else 0)
    if s < 5:
        return C_FAR * (7 + s - 2)
    if s > 11:
        return C_FAR * (10 + s - 12)
    return C_FAR * (s - 5)


def cap_of(s):
    return C_OWN if s == 0 else (C_NEAR if s in (1, 15) else C_FAR)


def iota(shape, dim):
    return lax.broadcasted_iota(jnp.int32, shape, dim).astype(F32)


def dot_nn(a, b):
    return lax.dot_general(a, b, (((1,), (0,)), ((), ())), preferred_element_type=F32)


def dot_nt(a, b):
    return lax.dot_general(a, b, (((1,), (1,)), ((), ())), preferred_element_type=F32)


def onehot(mask):
    return jnp.where(mask, 1.0, 0.0).astype(BF16)


def col_of(row):
    eye = iota((128, 128), 0) == iota((128, 128), 1)
    return jnp.sum(jnp.where(eye, row, 0.0), axis=1, keepdims=True)


def row_of(col):
    eye = iota((128, 128), 0) == iota((128, 128), 1)
    return jnp.sum(jnp.where(eye, col, 0.0), axis=0, keepdims=True)


def norm_rows(values, gain, offset):
    center = jnp.sum(values, axis=1, keepdims=True) * (1.0 / LAT)
    centered = values - center
    spread = jnp.sum(centered * centered, axis=1, keepdims=True) * (1.0 / LAT)
    return centered * lax.rsqrt(spread + EPSILON) * gain + offset


def silu(v):
    return v / (1.0 + jnp.exp(-v))


def kernel(
    recv_i, send_i, slot, cnt, el_hbm, grid_hbm, mesh_hbm,
    w0, w1, w2, w3, w4, w5, w6,
    b0, b1, b2, b3, b4, b5, b6, b7,
    mo_hbm, eo_hbm, flag_ref,
    el, grid, blk, wfull, tb, tbr, oh, tabt, t_ref, s_ref, sub_ref, r_ref, sd_ref, m_ref, rk_ref, o_ref,
    posb, posc, aq, bq, req_acc, req, reqr, m2_ref, posx,
    xc, sc, prec, metac, pre, srow, soh, serve, recvrows, scoh, msgb, mrecv, pcrow, eoc, xs, xr,
    mot, eot, summed, mrow, vecs, flagr,
    lsem, wlsem, t_ss, t_rs, w_ss, w_rs, f_ss, f_rs, q_ss, q_rs, g_ss, g_rs, m_ss, m_rs,
    x_ss, x_rs, mo_ss, mo_rs, fl_ss, fl_rs,
):
    p = lax.axis_index("patch")
    h = lax.axis_index("hidden")
    hf = h.astype(F32)
    pf = p.astype(F32)

    def hp(d):
        return lax.rem(h + d, NH)

    def pp(s):
        return lax.rem(p + s, NP)

    def remote(src, dst, ss, rs, dev):
        return pltpu.make_async_remote_copy(
            src_ref=src, dst_ref=dst, send_sem=ss, recv_sem=rs, device_id=dev, device_id_type=DEV
        )
    loads = [
        pltpu.make_async_copy(
            mesh_hbm.at[pl.ds(pl.multiple_of(h * SUB, SUB), SUB), :], blk, lsem.at[2]
        ),
        pltpu.make_async_copy(el_hbm, el, lsem.at[0]),
        pltpu.make_async_copy(grid_hbm, grid, lsem.at[1]),
    ]
    wsrc = (w0, w1, w2, w3, w4, w5, w6)
    wl = [pltpu.make_async_copy(wsrc[k], wfull.at[h, k], wlsem.at[k]) for k in range(7)]
    for c in wl:
        c.start()
    for c in loads:
        c.start()
    barrier = pltpu.get_barrier_semaphore()
    for d in range(1, NH):
        pl.semaphore_signal(barrier, inc=1, device_id=(p, hp(d)), device_id_type=DEV)
    for s in range(1, NP):
        pl.semaphore_signal(barrier, inc=1, device_id=(pp(s), h), device_id_type=DEV)
    i128 = iota((128, 128), 0)
    i256 = iota((256, 128), 0)
    vt = slot[...].astype(F32).T
    va = jnp.floor(vt * (1.0 / 256.0))
    vb = (vt - va * 256.0).astype(BF16)
    va = (va - 256.0).astype(BF16)
    tabt[512:768, :] = jnp.zeros((256, 256), BF16)
    for k in range(3):
        n = min(256, TAB - 256 * k)
        tabt[256 * k : 256 * k + 128, 0:n] = va[:, 256 * k : 256 * k + n]
        tabt[256 * k + 128 : 256 * k + 256, 0:n] = vb[:, 256 * k : 256 * k + n]

    def lookup(b, _):
        rr = recv_i[pl.ds(pl.multiple_of(b * 8, 8), 8), :]
        rhi = (lax.shift_right_logical(rr, 7) & 255).astype(F32)
        rtop = lax.shift_right_logical(rr, 15).astype(F32)
        rlo = (rr & 127).astype(F32)
        for k in range(8):
            oh[:, 128 * k : 128 * (k + 1)] = onehot(i256 == rhi[k : k + 1, :])
        pair = dot_nn(tabt[...], oh[...])
        for k in range(8):
            lanes = slice(128 * k, 128 * (k + 1))
            t0 = rtop[k : k + 1, :] == 0.0
            t1 = rtop[k : k + 1, :] == 1.0
            pa = jnp.where(t0, pair[0:128, lanes], jnp.where(t1, pair[256:384, lanes], pair[512:640, lanes]))
            pb = jnp.where(t0, pair[128:256, lanes], jnp.where(t1, pair[384:512, lanes], pair[640:768, lanes]))
            t_ref[pl.ds(b * 8 + k, 1), :] = jnp.sum(
                jnp.where(i128 == rlo[k : k + 1, :], (pa + 256.0) * 256.0 + pb, 0.0), axis=0, keepdims=True
            )
        return 0

    lax.fori_loop(0, 8, lookup, 0)
    for k, b in enumerate((b0, b1, b2, b3, b4, b5, b6, b7)):
        tb[k : k + 1, 0:LW] = b[...]
        tb[k : k + 1, LW:128] = b[...]
    for c in wl:
        c.wait()
    pl.semaphore_wait(barrier, NH - 1 + NP - 1)
    t_copies = [
        remote(tb, tbr.at[h], t_ss.at[d], t_rs.at[d], (p, hp(d))) for d in range(1, NH)
    ]
    for c in t_copies:
        c.start()
    tbr[h] = tb[...]
    parity = lax.rem(h, 2)
    partner = h + 1 - 2 * parity
    ahead = 2 - 4 * parity
    w_copies = []

    def along(part, i):
        lo, n = ((0, 4), (4, 3))[part]
        src_h, dst_h = ((h, h + 2), (h, h + NH - 2), (h - ahead + NH, h + ahead + NH))[i]
        ref = wfull.at[lax.rem(src_h, NH), pl.ds(lo, n)]
        return remote(ref, ref, w_ss.at[part * 4 + i], w_rs.at[part * 4 + i], (p, lax.rem(dst_h, NH)))

    def arrived(part, i):
        lo, n = ((0, 4), (4, 3))[part]
        ref = wfull.at[lax.rem(h + (NH - 2, 2, 4)[i], NH), pl.ds(lo, n)]
        remote(ref, ref, w_ss.at[part * 4 + i], w_rs.at[part * 4 + i], (p, partner)).wait_recv()

    def across(part, i, base):
        lo, n = ((0, 4), (4, 3))[part]
        ref = wfull.at[lax.rem(base + (0, NH - 2, 2, 4)[i], NH), pl.ds(lo, n)]
        return remote(ref, ref, f_ss.at[part * 4 + i], f_rs.at[part * 4 + i], (p, partner))

    def begin(c):
        c.start()
        w_copies.append(c)

    def stage0(part):
        begin(along(part, 0))
        begin(along(part, 1))
        begin(across(part, 0, h))

    def stage1(part):
        arrived(part, 0)
        arrived(part, 1)
        begin(along(part, 2))
        begin(across(part, 1, h))
        begin(across(part, 2, h))

    def stage2(part):
        arrived(part, 2)
        begin(across(part, 3, h))

    def weights_ready(part):
        for i in range(4):
            across(part, i, partner).wait_recv()

    stage0(0)

    tri = jnp.where(iota((128, 256), 1) < 128.0,
                    jnp.where(iota((128, 256), 0) < iota((128, 256), 1), 1.0, 0.0), 1.0).astype(BF16)
    i16 = iota((16, 128), 0)
    base16 = jnp.zeros((16, 128), F32)
    for s in range(NP):
        base16 = jnp.where(i16 == float(s), float(base_of(s)), base16)
    cap16 = jnp.where(i16 == 0.0, float(C_OWN), jnp.where((i16 == 1.0) | (i16 == 15.0), float(C_NEAR), float(C_FAR)))
    i48 = iota((48, 128), 0)
    tf = t_ref[...]
    q = jnp.floor((tf + 0.5) * (1.0 / MESH))
    rem = tf - q * MESH
    sub = jnp.floor((rem + 0.5) * (1.0 / SUB))
    r1 = rem - sub * SUB + 1.0
    shift = q - pf
    shift = jnp.where(shift < 0.0, shift + NP, shift)
    eidx = lax.broadcasted_iota(jnp.int32, (64, 128), 0) * 128 + lax.broadcasted_iota(jnp.int32, (64, 128), 1)
    live = eidx < cnt[0]
    own = live & (sub == hf)
    s_ref[...] = jnp.where(own, shift, -1.0)
    r_ref[...] = r1
    sd_ref[...] = (send_i[...] - p * GRID).astype(F32)
    spread = jnp.where(live, sub, lax.rem(eidx, NH).astype(F32))
    sub_ref[...] = spread
    o_ref[...] = dot_nn(onehot(spread == hf), tri)

    def mark(b, _):
        st = s_ref[pl.ds(pl.multiple_of(b * 8, 8), 8), :]
        for k in range(8):
            m_ref[pl.ds(pl.multiple_of(b * 128 + 16 * k, 16), 16), :] = onehot(i16 == st[k : k + 1, :])
        return 0

    lax.fori_loop(0, 8, mark, 0)
    rk_ref[...] = dot_nn(m_ref[...], tri)
    def place(b, carry):
        counts, most = carry
        b8 = pl.ds(pl.multiple_of(b * 8, 8), 8)
        st = s_ref[b8, :]
        rt = r_ref[b8, :]
        ot = o_ref[b8, :]
        sb = sub_ref[b8, :]
        rowcount = jnp.zeros((1, 128), F32)
        pbs, pcs = [], []
        vhi = jnp.floor(rt * (1.0 / 256.0))
        vlo = rt - vhi * 256.0
        for k in range(8):
            i0 = pl.ds(pl.multiple_of(b * 128 + 16 * k, 16), 16)
            rk = rk_ref[i0, :]
            mk = m_ref[i0, :].astype(F32)
            rank = rk[:, :128] + counts
            counts = counts + rk[:, 128:]
            isown = st[k : k + 1, :] >= 0.0
            pb = jnp.sum(mk * (base16 + rank), axis=0, keepdims=True)
            rk1 = jnp.sum(mk * rank, axis=0, keepdims=True)
            pbs.append(jnp.where(isown, pb, -1.0))
            pcs.append(jnp.where(sb[k : k + 1, :] == hf, ot[k : k + 1, :128] + rowcount, -1.0))
            rowcount = rowcount + ot[k : k + 1, 128:]
            qhi0 = jnp.floor(rk1 * (1.0 / 128.0))
            qlo = rk1 - qhi0 * 128.0
            qhi = jnp.where(isown & (qhi0 < 3.0), st[k : k + 1, :] * 3.0 + qhi0, -1.0)
            hit = i48 == qhi
            lanes = pl.ds(pl.multiple_of(b * 1024 + 128 * k, 128), 128)
            aq[0:48, lanes] = jnp.where(hit, vhi[k : k + 1, :], 0.0).astype(BF16)
            aq[48:96, lanes] = jnp.where(hit, vlo[k : k + 1, :], 0.0).astype(BF16)
            bq[:, lanes] = onehot(i128 == qlo)
        for k in range(8):
            posb[pl.ds(b * 8 + k, 1), :] = pbs[k]
            posc[pl.ds(b * 8 + k, 1), :] = pcs[k]
        return counts, jnp.maximum(most, rowcount)

    counts, most = lax.fori_loop(0, 8, place, (jnp.zeros((16, 128), F32), jnp.zeros((1, 128), F32)))
    req_acc[...] = dot_nt(aq[...], bq[...])
    over = jnp.max(jnp.where(counts > cap16, 1.0, 0.0), axis=0, keepdims=True)
    over = jnp.maximum(over, jnp.where(most > float(C_BLK), 1.0, 0.0))
    for s in range(NP):
        req[s, 0:3, :] = req_acc[3 * s : 3 * s + 3, :] * 256.0 + req_acc[48 + 3 * s : 48 + 3 * s + 3, :] - 1.0
        req[s, 3:7, :] = jnp.full((4, 128), -1.0, F32)
        req[s, 7:8, :] = over
    q_copies = [
        remote(req.at[s], reqr.at[s], q_ss.at[s], q_rs.at[s], (pp(s), h)) for s in range(1, NP)
    ]
    for c in q_copies:
        c.start()
    reqr[0] = req[0]
    for c in loads:
        c.wait()
    ic = iota((C_BLK, 128), 0)

    def compact(b, _):
        b8 = pl.ds(pl.multiple_of(b * 8, 8), 8)
        pct = posc[b8, :]
        pbt = posb[b8, :] + 1.0
        sdt = sd_ref[b8, :]
        at_b = jnp.zeros((C_BLK, 128), F32)
        at_s = jnp.zeros((C_BLK, 128), F32)
        for k in range(8):
            hit = ic == pct[k : k + 1, :]
            oh[0:C_BLK, 128 * k : 128 * (k + 1)] = onehot(hit)
            at_b = at_b + jnp.where(hit, pbt[k : k + 1, :], 0.0)
            at_s = at_s + jnp.where(hit, sdt[k : k + 1, :], 0.0)
        rows = pl.ds(pl.multiple_of(b * C_BLK, 16), C_BLK)
        xc[rows, :] = dot_nn(oh[0:C_BLK, :], el[pl.ds(pl.multiple_of(b * BLK, BLK), BLK), :]).astype(BF16)
        lanes = lax.broadcasted_iota(jnp.int32, (C_BLK, 128), 1)
        metac[rows, :] = jnp.where(
            lanes < 64,
            jnp.sum(at_b, axis=1, keepdims=True) - 1.0,
            jnp.sum(at_s, axis=1, keepdims=True),
        )
        return 0

    lax.fori_loop(0, EARLY, compact, 0)
    for k in range(NCOMP // 128):
        pcrow[:, 128 * k : 128 * (k + 1)] = jnp.broadcast_to(
            row_of(metac[128 * k : 128 * (k + 1), 0:1]), (8, 128)
        )
    for c in q_copies:
        c.wait_recv()
    stage1(0)
    for s in range(NP):
        b, c = base_of(s), cap_of(s)
        for j in range(-(-c // 128)):
            n = min(128, c - 128 * j)
            srow[0:1, b + 128 * j : b + 128 * j + n] = reqr[s, j : j + 1, 0:n]
    flag_p = jnp.max(reqr[:, 7, :], axis=0, keepdims=True)
    flagr[h] = jnp.broadcast_to(flag_p, (8, 128))
    il640 = iota((128, SUB), 1)
    for k in range(NROW // 128):
        soh[128 * k : 128 * (k + 1), :] = onehot(il640 == col_of(srow[0:1, 128 * k : 128 * (k + 1)]))
    def serve_rows(c, _):
        rows = pl.ds(pl.multiple_of(c * 2 * MCH, 16), 2 * MCH)
        serve[rows, :] = dot_nn(soh[rows, :], blk[...]).astype(BF16)
        return 0

    lax.fori_loop(0, NROW // (2 * MCH), serve_rows, 0)
    order = sum(GROUPS, ())
    g_copies = []
    for s in order:
        rows = pl.ds(base_of(s), cap_of(s))
        c = remote(
            serve.at[rows], recvrows.at[rows], g_ss.at[s], g_rs.at[s], (lax.rem(p + NP - s, NP), h)
        )
        c.start()
        g_copies.append(c)
    ownr = slice(base_of(0), base_of(0) + C_OWN)
    recvrows[ownr, :] = serve[ownr, :]
    fl_copies = [
        remote(flagr.at[h], flagr.at[h], fl_ss.at[d], fl_rs.at[d], (p, hp(d))) for d in range(1, NH)
    ]
    for c in fl_copies:
        c.start()
    isub = iota((SUB, 128), 0)
    for k in range(NROW // 128):
        scoh[:, 128 * k : 128 * (k + 1)] = onehot(isub == srow[0:1, 128 * k : 128 * (k + 1)])
    def gather_senders(c, _):
        rows = pl.ds(pl.multiple_of(c * SCH, 16), SCH)
        pick = metac[rows, 64:65]
        sc[rows, :] = dot_nn(onehot(iota((SCH, GRID), 1) == pick), grid[...]).astype(BF16)
        return 0

    lax.fori_loop(0, NCOMP // SCH, gather_senders, 0)
    stage2(0)
    stage0(1)
    weights_ready(0)
    for c in t_copies:
        c.wait_recv()
    lane = lax.broadcasted_iota(jnp.int32, (8, 128), 1)
    for j in range(4):
        even, odd = tbr[2 * j], tbr[2 * j + 1]
        vecs[:, 128 * j : 128 * (j + 1)] = jnp.where(lane < LW, even, odd)

    def full(k):
        return wfull[:, k].reshape(LAT, LAT)

    def first(c, _):
        rows = pl.ds(pl.multiple_of(c * FCH, 16), FCH)
        prec[rows, :] = (dot_nt(xc[rows, :], full(0)) + dot_nt(sc[rows, :], full(1)) + vecs[0:1, :]).astype(BF16)
        return 0

    lax.fori_loop(0, NCOMP // FCH, first, 0)

    def arrange(c, _):
        rows = pl.ds(pl.multiple_of(c * PCH, 16), PCH)
        j0 = (c * PCH).astype(F32)
        pre[rows, :] = dot_nn(onehot(iota((PCH, NCOMP), 0) + j0 == pcrow[0:1, :]), prec[...])
        return 0

    lax.fori_loop(0, NROW // PCH, arrange, 0)

    def mlp(start, n):
        rows = slice(start, start + n)
        v = pre[rows, :] + dot_nt(recvrows[rows, :], full(2))
        hid = silu(v).astype(BF16)
        msg = norm_rows(dot_nn(hid, full(3)) + vecs[1:2, :], vecs[2:3, :], vecs[3:4, :])
        msgb[rows, :] = msg.astype(BF16)
    stage1(1)
    mlp(base_of(0), C_OWN // 2)
    mlp(base_of(0) + C_OWN // 2, C_OWN // 2)
    mrecv[ownr, :] = msgb[ownr, :]
    m_copies = []
    g_wait = dict(zip(order, g_copies))
    for gi, group in enumerate(GROUPS):
        for s in group:
            g_wait[s].wait_recv()
        start = base_of(group[0])
        n = sum(cap_of(s) for s in group)
        mlp(start, n // 2)
        mlp(start + n // 2, n - n // 2)
        for s in group:
            rows = pl.ds(base_of(s), cap_of(s))
            c = remote(msgb.at[rows], mrecv.at[rows], m_ss.at[s], m_rs.at[s], (pp(s), h))
            c.start()
            m_copies.append(c)
    stage2(1)


    def scatter_block(c, _):
        rows = pl.ds(pl.multiple_of(c * SCH, 16), SCH)
        perm = onehot(iota((SCH, NROW), 1) == metac[rows, 0:1])
        eoc[rows, :] = (xc[rows, :].astype(F32) + dot_nn(perm, msgb[...])).astype(BF16)
        return 0

    lax.fori_loop(0, NCOMP // SCH, scatter_block, 0)
    low = lax.broadcasted_iota(jnp.int32, (HALF, 128), 1) < LW
    for j in range(4):
        cols = slice(128 * j, 128 * (j + 1))
        top = eoc[0:HALF, cols].astype(F32)
        bottom = eoc[HALF:NCOMP, cols].astype(F32)
        xs[2 * j] = jnp.where(low, top, pltpu.roll(bottom, LW, 1)).astype(BF16)
        xs[2 * j + 1] = jnp.where(low, pltpu.roll(top, LW, 1), bottom).astype(BF16)
    x_copies = []
    for half in range(2):
        part = pl.ds(half * HALF // 2, HALF // 2)
        for d in range(1, NH):
            i = half * 8 + d
            c = remote(xs.at[hp(d), part], xr.at[h, part], x_ss.at[i], x_rs.at[i], (p, hp(d)))
            c.start()
            x_copies.append(c)
    xr[h] = xs[h]

    i8 = iota((8, 128), 0)

    def mark2(b, _):
        st = sub_ref[pl.ds(pl.multiple_of(b * 8, 8), 8), :]
        for k in range(8):
            m2_ref[pl.ds(pl.multiple_of(b * 64 + 8 * k, 8), 8), :] = jnp.where(i8 == st[k : k + 1, :], 1.0, 0.0)
        return 0

    lax.fori_loop(0, 8, mark2, 0)
    rk_ref[0:512, :] = dot_nn(m2_ref[...].astype(BF16), tri)

    def place2(b, _):
        seen = jnp.zeros((8, 128), F32)
        for k in range(8):
            i0 = pl.ds(pl.multiple_of(b * 64 + 8 * k, 8), 8)
            rk = rk_ref[i0, :]
            rank = rk[:, :128] + seen
            seen = seen + rk[:, 128:]
            posx[pl.ds(b * 8 + k, 1), :] = jnp.sum(
                m2_ref[i0, :] * (i8 * float(C_BLK) + rank), axis=0, keepdims=True
            )
        return 0

    lax.fori_loop(0, 8, place2, 0)
    lane_low = lax.broadcasted_iota(jnp.int32, (UCH, 128), 1) < LW

    def rows_arrived(half):
        for d in range(1, NH):
            src = xr.at[lax.rem(h + NH - d, NH), pl.ds(half * HALF // 2, HALF // 2)]
            remote(src, src, x_ss.at[half * 8 + d], x_rs.at[half * 8 + d], (p, hp(d))).wait_recv()

    def edge_rows(t, _):
        b = t // (BLK // UCH)
        c = t - b * (BLK // UCH)
        x2 = xr[:, pl.ds(pl.multiple_of(b * C_BLK, 16), C_BLK), :].reshape(NCOMP, 128)
        x2 = jnp.concatenate([x2[0:HALF], x2[HALF:NCOMP]], axis=1)
        perms = []
        tops = []
        for block in (b, b + 4):
            for k in range(UCH // 128):
                col = col_of(posx[pl.ds(block * 8 + c * (UCH // 128) + k, 1), :])
                top = col >= float(HALF)
                tops.append(jnp.broadcast_to(jnp.where(top, 1.0, 0.0), (128, 128)))
                perms.append(onehot(iota((128, HALF), 1) == jnp.where(top, col - float(HALF), col)))
        got = dot_nn(jnp.concatenate(perms, axis=0), x2)
        got = jnp.where(jnp.concatenate(tops, axis=0) > 0.5, got[:, 128:256], got[:, 0:128])
        both = jnp.where(lane_low, got[0:UCH], got[UCH : 2 * UCH]).T.astype(BF16)
        eot[:, pl.ds(pl.multiple_of(b * BLK + c * UCH, 128), UCH)] = both[0:LW]
        eot[:, pl.ds(pl.multiple_of((b + 4) * BLK + c * UCH, 128), UCH)] = both[LW:128]
        return 0

    per_half = 2 * (BLK // UCH)

    for c in m_copies:
        c.wait_recv()
    weights_ready(1)
    for c in range(2):
        rows = slice(c * SUB // 2, (c + 1) * SUB // 2)
        summed[rows, :] = dot_nn(scoh[rows, :], mrecv[...]).astype(BF16)

    def mesh(c, _):
        rows = pl.ds(pl.multiple_of(c * (SUB // 2), 16), SUB // 2)
        x = blk[rows, :]
        v = dot_nt(x, full(4)) + dot_nt(summed[rows, :], full(5)) + vecs[4:5, :]
        hid = silu(v).astype(BF16)
        upd = norm_rows(dot_nn(hid, full(6)) + vecs[5:6, :], vecs[6:7, :], vecs[7:8, :])
        mrow[rows, :] = x.astype(F32) + upd
        return 0

    lax.fori_loop(0, 2, mesh, 0)

    def turn(c, _):
        rows = pl.ds(pl.multiple_of(c * 128, 128), 128)
        mot[:, rows] = mrow[rows, :].T.astype(BF16)
        return 0

    lax.fori_loop(0, SUB // 128, turn, 0)
    mo_copies = []
    at_mesh = pl.ds(pl.multiple_of(h * SUB, 128), SUB)
    for d in range(1, NH):
        c = remote(
            mot.at[pl.ds(pl.multiple_of(hp(d) * LW, LW), LW), :], mo_hbm.at[:, at_mesh],
            mo_ss.at[d], mo_rs.at[d], (p, hp(d)),
        )
        c.start()
        mo_copies.append(c)
    mo_own = pltpu.make_async_copy(
        mot.at[pl.ds(pl.multiple_of(h * LW, LW), LW), :], mo_hbm.at[:, at_mesh], lsem.at[3]
    )
    mo_own.start()
    rows_arrived(0)
    lax.fori_loop(0, per_half, edge_rows, 0)
    rows_arrived(1)
    lax.fori_loop(per_half, 2 * per_half, edge_rows, 0)
    eo_own = pltpu.make_async_copy(eot, eo_hbm, lsem.at[4])
    eo_own.start()
    for d in range(1, NH):
        src = lax.rem(h + NH - d, NH)
        remote(flagr.at[src], flagr.at[src], fl_ss.at[d], fl_rs.at[d], (p, hp(d))).wait_recv()
    flag_ref[...] = jnp.max(flagr[...], axis=0)
    for c in t_copies + w_copies + q_copies + g_copies + fl_copies + m_copies + x_copies + mo_copies:
        c.wait_send()
    for d in range(1, NH):
        src_h = lax.rem(h + NH - d, NH)
        at_m = pl.ds(pl.multiple_of(src_h * SUB, 128), SUB)
        remote(mo_hbm.at[:, at_m], mo_hbm.at[:, at_m], mo_ss.at[d], mo_rs.at[d], (p, hp(d))).wait_recv()
    mo_own.wait()
    eo_own.wait()


def sparse_step(grid_latent, mesh_latent, edge_latent, senders, receivers, mesh_slot, edge_counts,
                w_edge, w_sender, w_receiver, edge_bias, w_edge_out, edge_out_bias, edge_gain, edge_shift,
                w_mesh_in, w_message_in, mesh_bias, w_mesh_out, mesh_out_bias, mesh_gain, mesh_shift):
    V = pltpu.VMEM
    vm = pl.BlockSpec(memory_space=pltpu.VMEM)
    anyspec = pl.BlockSpec(memory_space=pl.ANY)
    weights = (w_edge.T, w_sender.T, w_receiver.T, w_edge_out, w_mesh_in.T, w_message_in.T, w_mesh_out)
    vectors = tuple(v.reshape(1, LW) for v in (
        edge_bias, edge_out_bias, edge_gain, edge_shift, mesh_bias, mesh_out_bias, mesh_gain, mesh_shift))
    dma = pltpu.SemaphoreType.DMA
    scratch = [
        V((EDGE, LAT), BF16), V((GRID, LAT), BF16), V((SUB, LAT), BF16), V((NH, 7, LW, LAT), BF16),
        V((8, 128), F32), V((NH, 8, 128), F32), V((256, 1024), BF16), V((768, 256), BF16), V((64, 128), F32),
        V((64, 128), F32), V((64, 128), F32), V((64, 128), F32), V((64, 128), F32),
        V((1024, 128), BF16), V((1024, 256), F32), V((64, 256), F32),
        V((64, 128), F32), V((64, 128), F32), V((96, EDGE), BF16), V((128, EDGE), BF16),
        V((96, 128), F32), V((NP, 8, 128), F32), V((NP, 8, 128), F32),
        V((512, 128), F32), V((64, 128), F32),
        V((NCOMP, LAT), BF16), V((NCOMP, LAT), BF16), V((NCOMP, LAT), BF16), V((NCOMP, 128), F32), V((NROW, LAT), F32),
        V((8, NROW), F32), V((NROW, SUB), BF16), V((NROW, LAT), BF16), V((NROW, LAT), BF16),
        V((SUB, NROW), BF16), V((NROW, LAT), BF16), V((NROW, LAT), BF16),
        V((8, NCOMP), F32), V((NCOMP, LAT), BF16), V((NH, HALF, 128), BF16), V((NH, HALF, 128), BF16),
        V((LAT, SUB), BF16), V((LW, EDGE), BF16), V((SUB, LAT), BF16), V((SUB, LAT), F32), V((8, LAT), F32), V((NH, 8, 128), F32),
        dma((5,)), dma((7,)), dma((8,)), dma((8,)), dma((8,)), dma((8,)), dma((8,)), dma((8,)),
        dma((16,)), dma((16,)), dma((16,)), dma((16,)), dma((16,)), dma((16,)),
        dma((16,)), dma((16,)), dma((8,)), dma((8,)), dma((8,)), dma((8,)),
    ]
    mo_t, eo_t, flag = pl.pallas_call(
        kernel,
        out_shape=(
            jax.ShapeDtypeStruct((LW, MESH), BF16),
            jax.ShapeDtypeStruct((LW, EDGE), BF16),
            jax.ShapeDtypeStruct((8, 128), F32),
        ),
        in_specs=[vm, vm, vm, pl.BlockSpec(memory_space=pltpu.SMEM), anyspec, anyspec, anyspec]
        + [anyspec] * 7 + [vm] * 8,
        out_specs=(anyspec, anyspec, vm),
        scratch_shapes=scratch,
        compiler_params=pltpu.CompilerParams(
            collective_id=0, has_side_effects=True, vmem_limit_bytes=62 * 1024 * 1024
        ),
        name="encoder",
    )(receivers.reshape(64, 128), senders.reshape(64, 128), mesh_slot.reshape(TAB, 128), edge_counts,
      edge_latent, grid_latent, mesh_latent, *weights, *vectors)
    return mo_t, eo_t, flag


def from_everyone(x, axis):
    copies = jnp.broadcast_to(x, (lax.axis_size(axis), *x.shape))
    return lax.all_to_all(copies, axis, split_axis=0, concat_axis=0, tiled=True)


def total_of(x, axis):
    return from_everyone(x, axis).sum(axis=0)


def scatter_columns(x):
    parts = x.astype(BF16).reshape(x.shape[0], NH, LW).transpose(1, 0, 2)
    got = lax.all_to_all(parts, "hidden", split_axis=0, concat_axis=0, tiled=True)
    return got.astype(F32).sum(axis=0)


def normalize(values, gain, offset):
    center = total_of(jnp.sum(values, axis=1), "hidden") / LAT
    centered = values - center[:, None]
    spread = total_of(jnp.sum(centered * centered, axis=1), "hidden") / LAT
    return centered * lax.rsqrt(spread + EPSILON)[:, None] * gain + offset


def general_step(grid_latent, mesh_latent, edge_latent, senders, receivers, mesh_slot, edge_counts,
                 w_edge, w_sender, w_receiver, edge_bias, w_edge_out, edge_out_bias, edge_gain, edge_shift,
                 w_mesh_in, w_message_in, mesh_bias, w_mesh_out, mesh_out_bias, mesh_gain, mesh_shift):
    column = lax.axis_index("hidden")
    target = jnp.take(mesh_slot, receivers)
    sender = senders - lax.axis_index("patch") * GRID
    live = (jnp.arange(EDGE, dtype=jnp.int32) < edge_counts[0]).astype(F32)
    proj = jnp.dot(mesh_latent, w_receiver, preferred_element_type=F32).astype(BF16)
    table = from_everyone(proj, "patch").reshape(NP * MESH, LW)
    edge_pre = (
        jnp.dot(edge_latent, w_edge, preferred_element_type=F32)
        + jnp.dot(jnp.take(grid_latent, sender, axis=0), w_sender, preferred_element_type=F32)
        + jnp.take(table, target, axis=0).astype(F32)
        + edge_bias
    )
    hid = silu(edge_pre).astype(BF16)
    edge_sum = scatter_columns(jnp.dot(hid, w_edge_out, preferred_element_type=F32)) + edge_out_bias
    message = normalize(edge_sum, edge_gain, edge_shift) * live[:, None]
    cols = lax.dynamic_slice_in_dim(edge_latent, column * LW, LW, 1)
    edge_out = (cols.astype(F32) + message).astype(BF16)
    sums = jax.ops.segment_sum(message, target, num_segments=NP * MESH).astype(BF16)
    got = lax.all_to_all(sums.reshape(NP, MESH, LW), "patch", split_axis=0, concat_axis=0, tiled=True)
    own = got.astype(F32).sum(axis=0).astype(BF16)
    summed = from_everyone(own, "hidden").transpose(1, 0, 2).reshape(MESH, LAT)
    mesh_pre = (
        jnp.dot(mesh_latent, w_mesh_in, preferred_element_type=F32)
        + jnp.dot(summed, w_message_in, preferred_element_type=F32)
        + mesh_bias
    )
    hid = silu(mesh_pre).astype(BF16)
    mesh_sum = scatter_columns(jnp.dot(hid, w_mesh_out, preferred_element_type=F32)) + mesh_out_bias
    update = normalize(mesh_sum, mesh_gain, mesh_shift)
    cols = lax.dynamic_slice_in_dim(mesh_latent, column * LW, LW, 1)
    return (cols.astype(F32) + update).astype(BF16).T, edge_out.T


def step(*args):
    mo_t, eo_t, flag = sparse_step(*args)

    def again(state):
        mo, eo = general_step(*args)
        return jnp.zeros_like(state[0]), mo, eo

    mo_t, eo_t = lax.cond(flag[0, 0] > 0.5, lambda: general_step(*args), lambda: (mo_t, eo_t))
    return mo_t.T, eo_t.T


def solution(mesh):
    return jax.shard_map(
        step,
        mesh=mesh,
        in_specs=(
            P("patch", None), P("patch", None), P("patch", None), P("patch"), P("patch"), P(), P("patch"),
            P(None, "hidden"), P(None, "hidden"), P(None, "hidden"), P("hidden"), P("hidden", None),
            P("hidden"), P("hidden"), P("hidden"), P(None, "hidden"), P(None, "hidden"), P("hidden"),
            P("hidden", None), P("hidden"), P("hidden"), P("hidden"),
        ),
        out_specs=(P("patch", "hidden"), P("patch", "hidden")),
        check_vma=False,
    )
```

time: 104 us -> 80.5 us (0.77)
  Pallas kernels: 98.2 us -> 75.1 us
    pallas_call x1, Pallas kernels: 98.2 us -> 75.1 us  [sparse_step(): pl.pallas_call(kernel, out_shape=(jax.ShapeDtypeStruct((LW, MESH), BF16),...]
where the time goes in v2:
time: 80.5 us; the launch traced here: 80.4 us
  Pallas kernels  75.1 us (93%)
  local copies, waits for them, and re-layouts  3.01 us (4%)
  between operations  1.96 us (2%)
    pallas_call x1, Pallas kernels, sparse_step(): pl.pallas_call(kernel, out_shape=(jax.ShapeDtypeStruct((LW, MESH), BF16),...  75.1 us
    unnamed x4, local copies, waits for them, and re-layouts  1.81 us

profile of v2, /device:TPU:1, one launch (start us, length us, event | category | flops | bytes accessed | tf_op | source)
XLA Modules:
  0.0 80.4 jit_solution(13716846298461651620)
XLA Ops:
  1.3 0.0 copy-start
  1.3 75.1 %encoder.1 = (bf16[64,5120]{1,0:T(8,128)(2,1)S(1)}, bf16[64,8192]{1,0:T(8,128)(2,1)S(1)}, f32[8,128]{1,0:T(8,128)}) custom-call(s32[64,128]{1,0:T(8,128)} %bitcast.57, s32[64,128]{1,0:T(8,128)} %bitcast.58, s32[640,128]{1,0:T(8,128)} %bitcast.49, s32[1]{0:T(128)S(6)} %copy.142.cnt, bf16[8192,512]{1,0:T(8,128)(2,1)} %el_hbm.1, bf16[3072,512]{1,0:T(8,128)(2,1)} %grid_hbm.1, ...), custom_call_target="tpu_custom_call" | custom-call | tf_op jit(solution)/shard_map/encoder/pallas_call | solution.py:600
  76.4 1.2 %slice.3 = f32[1,1]{1,0:T(1,128)} slice(f32[8,128]{1,0:T(8,128)} %get-tuple-element.77), slice={[0:1], [0:1]} | slice | bytes 8 | tf_op jit(solution)/shard_map/slice | solution.py:685
  78.3 0.0 copy-done
  78.3 0.3 conditional.1
  78.6 0.8 %copy.143 = bf16[5120,64]{0,1:T(8,128)(2,1)} copy(bf16[5120,64]{0,1:T(8,128)(2,1)S(1)} %bitcast.56) | data formatting | bytes 1310720
  79.4 1.0 %copy.144 = bf16[8192,64]{0,1:T(8,128)(2,1)} copy(bf16[8192,64]{0,1:T(8,128)(2,1)S(1)} %bitcast.55) | data formatting | bytes 2097152
Async XLA Ops:
  1.3 77.0 %copy-start = (s32[81920]{0:T(1024)S(1)}, s32[81920]{0:T(1024)}, u32[]{:S(2)}) copy-start(s32[81920]{0:T(1024)} %param.29) | copy-start | bytes 983044

commit v3 on v2

--- a/solution.py
+++ b/solution.py
@@ -30,6 +30,7 @@
 UCH = 512
 HALF = NCOMP // 2
 DEV = pl.DeviceIdType.MESH
+PARTS = ((0, 2), (2, 2), (4, 3))
 GROUPS = ((5, 6, 7, 8, 9, 10, 11), (2, 3, 4, 12, 13, 14), (1, 15))
 
 
@@ -90,13 +91,12 @@
     recv_i, send_i, slot, cnt, el_hbm, grid_hbm, mesh_hbm,
     w0, w1, w2, w3, w4, w5, w6,
     b0, b1, b2, b3, b4, b5, b6, b7,
-    mo_hbm, eo_hbm, flag_ref,
+    mo_hbm, eo_hbm, flag_hbm,
     el, grid, blk, wfull, tb, tbr, oh, tabt, t_ref, s_ref, sub_ref, r_ref, sd_ref, m_ref, rk_ref, o_ref,
     posb, posc, aq, bq, req_acc, req, reqr, m2_ref, posx,
     xc, sc, prec, metac, pre, srow, soh, serve, recvrows, scoh, msgb, mrecv, pcrow, eoc, xs, xr,
-    mot, eot, summed, mrow, vecs, flagr,
-    lsem, wlsem, t_ss, t_rs, w_ss, w_rs, f_ss, f_rs, q_ss, q_rs, g_ss, g_rs, m_ss, m_rs,
-    x_ss, x_rs, mo_ss, mo_rs, fl_ss, fl_rs,
+    mot, eot, mpre, mrow, vecs, flagr, flag_v,
+    lsem, snd, rcv,
 ):
     p = lax.axis_index("patch")
     h = lax.axis_index("hidden")
@@ -113,6 +113,12 @@
         return pltpu.make_async_remote_copy(
             src_ref=src, dst_ref=dst, send_sem=ss, recv_sem=rs, device_id=dev, device_id_type=DEV
         )
+    def got(ref, i):
+        remote(ref, ref, snd.at[0], rcv.at[i], (p, h + 1 - 2 * lax.rem(h, 2))).wait_recv()
+
+    def sent(ref, i):
+        remote(ref, ref, snd.at[i], rcv.at[0], (p, h + 1 - 2 * lax.rem(h, 2))).wait_send()
+
     loads = [
         pltpu.make_async_copy(
             mesh_hbm.at[pl.ds(pl.multiple_of(h * SUB, SUB), SUB), :], blk, lsem.at[2]
@@ -121,7 +127,7 @@
         pltpu.make_async_copy(grid_hbm, grid, lsem.at[1]),
     ]
     wsrc = (w0, w1, w2, w3, w4, w5, w6)
-    wl = [pltpu.make_async_copy(wsrc[k], wfull.at[h, k], wlsem.at[k]) for k in range(7)]
+    wl = [pltpu.make_async_copy(wsrc[k], wfull.at[h, k], lsem.at[3]) for k in range(7)]
     for c in wl:
         c.start()
     for c in loads:
@@ -143,6 +149,9 @@
         tabt[256 * k : 256 * k + 128, 0:n] = va[:, 256 * k : 256 * k + n]
         tabt[256 * k + 128 : 256 * k + 256, 0:n] = vb[:, 256 * k : 256 * k + n]
 
+    parity = lax.rem(h, 2)
+    partner = h + 1 - 2 * parity
+
     def lookup(b, _):
         rr = recv_i[pl.ds(pl.multiple_of(b * 8, 8), 8), :]
         rhi = (lax.shift_right_logical(rr, 7) & 255).astype(F32)
@@ -162,39 +171,39 @@
             )
         return 0
 
-    lax.fori_loop(0, 8, lookup, 0)
+    lax.fori_loop(parity * 4, parity * 4 + 4, lookup, 0)
     for k, b in enumerate((b0, b1, b2, b3, b4, b5, b6, b7)):
         tb[k : k + 1, 0:LW] = b[...]
         tb[k : k + 1, LW:128] = b[...]
-    for c in wl:
-        c.wait()
+    pltpu.make_async_copy(wfull.at[h], wfull.at[h], lsem.at[3]).wait()
     pl.semaphore_wait(barrier, NH - 1 + NP - 1)
+    own_half = t_ref.at[pl.ds(pl.multiple_of(parity * 32, 32), 32), :]
+    other_half = t_ref.at[pl.ds(pl.multiple_of(32 - parity * 32, 32), 32), :]
+    swap = remote(own_half, own_half, snd.at[0], rcv.at[0], (p, partner))
+    swap.start()
     t_copies = [
-        remote(tb, tbr.at[h], t_ss.at[d], t_rs.at[d], (p, hp(d))) for d in range(1, NH)
+        remote(tb, tbr.at[h], snd.at[1], rcv.at[1], (p, hp(d))) for d in range(1, NH)
     ]
     for c in t_copies:
         c.start()
     tbr[h] = tb[...]
-    parity = lax.rem(h, 2)
-    partner = h + 1 - 2 * parity
     ahead = 2 - 4 * parity
     w_copies = []
 
     def along(part, i):
-        lo, n = ((0, 4), (4, 3))[part]
+        lo, n = PARTS[part]
         src_h, dst_h = ((h, h + 2), (h, h + NH - 2), (h - ahead + NH, h + ahead + NH))[i]
         ref = wfull.at[lax.rem(src_h, NH), pl.ds(lo, n)]
-        return remote(ref, ref, w_ss.at[part * 4 + i], w_rs.at[part * 4 + i], (p, lax.rem(dst_h, NH)))
+        return remote(ref, ref, snd.at[2], rcv.at[12 + 2 * part + i // 2], (p, lax.rem(dst_h, NH)))
 
     def arrived(part, i):
-        lo, n = ((0, 4), (4, 3))[part]
-        ref = wfull.at[lax.rem(h + (NH - 2, 2, 4)[i], NH), pl.ds(lo, n)]
-        remote(ref, ref, w_ss.at[part * 4 + i], w_rs.at[part * 4 + i], (p, partner)).wait_recv()
+        lo, n = PARTS[part]
+        got(wfull.at[0 : 2 - i, pl.ds(lo, n)], 12 + 2 * part + i)
 
     def across(part, i, base):
-        lo, n = ((0, 4), (4, 3))[part]
+        lo, n = PARTS[part]
         ref = wfull.at[lax.rem(base + (0, NH - 2, 2, 4)[i], NH), pl.ds(lo, n)]
-        return remote(ref, ref, f_ss.at[part * 4 + i], f_rs.at[part * 4 + i], (p, partner))
+        return remote(ref, ref, snd.at[3], rcv.at[18 + part], (p, partner))
 
     def begin(c):
         c.start()
@@ -207,20 +216,20 @@
 
     def stage1(part):
         arrived(part, 0)
-        arrived(part, 1)
         begin(along(part, 2))
         begin(across(part, 1, h))
         begin(across(part, 2, h))
 
     def stage2(part):
-        arrived(part, 2)
+        arrived(part, 1)
         begin(across(part, 3, h))
 
     def weights_ready(part):
-        for i in range(4):
-            across(part, i, partner).wait_recv()
+        lo, n = PARTS[part]
+        got(wfull.at[0:4, pl.ds(lo, n)], 18 + part)
 
     stage0(0)
+    stage0(1)
 
     tri = jnp.where(iota((128, 256), 1) < 128.0,
                     jnp.where(iota((128, 256), 0) < iota((128, 256), 1), 1.0, 0.0), 1.0).astype(BF16)
@@ -230,6 +239,7 @@
         base16 = jnp.where(i16 == float(s), float(base_of(s)), base16)
     cap16 = jnp.where(i16 == 0.0, float(C_OWN), jnp.where((i16 == 1.0) | (i16 == 15.0), float(C_NEAR), float(C_FAR)))
     i48 = iota((48, 128), 0)
+    got(other_half, 0)
     tf = t_ref[...]
     q = jnp.floor((tf + 0.5) * (1.0 / MESH))
     rem = tf - q * MESH
@@ -300,7 +310,7 @@
         req[s, 3:7, :] = jnp.full((4, 128), -1.0, F32)
         req[s, 7:8, :] = over
     q_copies = [
-        remote(req.at[s], reqr.at[s], q_ss.at[s], q_rs.at[s], (pp(s), h)) for s in range(1, NP)
+        remote(req.at[s], reqr.at[s], snd.at[4], rcv.at[2], (pp(s), h)) for s in range(1, NP)
     ]
     for c in q_copies:
         c.start()
@@ -331,134 +341,12 @@
         )
         return 0
 
-    lax.fori_loop(0, EARLY, compact, 0)
+    lax.fori_loop(0, 8, compact, 0)
+    stage1(0)
     for k in range(NCOMP // 128):
         pcrow[:, 128 * k : 128 * (k + 1)] = jnp.broadcast_to(
             row_of(metac[128 * k : 128 * (k + 1), 0:1]), (8, 128)
         )
-    for c in q_copies:
-        c.wait_recv()
-    stage1(0)
-    for s in range(NP):
-        b, c = base_of(s), cap_of(s)
-        for j in range(-(-c // 128)):
-            n = min(128, c - 128 * j)
-            srow[0:1, b + 128 * j : b + 128 * j + n] = reqr[s, j : j + 1, 0:n]
-    flag_p = jnp.max(reqr[:, 7, :], axis=0, keepdims=True)
-    flagr[h] = jnp.broadcast_to(flag_p, (8, 128))
-    il640 = iota((128, SUB), 1)
-    for k in range(NROW // 128):
-        soh[128 * k : 128 * (k + 1), :] = onehot(il640 == col_of(srow[0:1, 128 * k : 128 * (k + 1)]))
-    def serve_rows(c, _):
-        rows = pl.ds(pl.multiple_of(c * 2 * MCH, 16), 2 * MCH)
-        serve[rows, :] = dot_nn(soh[rows, :], blk[...]).astype(BF16)
-        return 0
-
-    lax.fori_loop(0, NROW // (2 * MCH), serve_rows, 0)
-    order = sum(GROUPS, ())
-    g_copies = []
-    for s in order:
-        rows = pl.ds(base_of(s), cap_of(s))
-        c = remote(
-            serve.at[rows], recvrows.at[rows], g_ss.at[s], g_rs.at[s], (lax.rem(p + NP - s, NP), h)
-        )
-        c.start()
-        g_copies.append(c)
-    ownr = slice(base_of(0), base_of(0) + C_OWN)
-    recvrows[ownr, :] = serve[ownr, :]
-    fl_copies = [
-        remote(flagr.at[h], flagr.at[h], fl_ss.at[d], fl_rs.at[d], (p, hp(d))) for d in range(1, NH)
-    ]
-    for c in fl_copies:
-        c.start()
-    isub = iota((SUB, 128), 0)
-    for k in range(NROW // 128):
-        scoh[:, 128 * k : 128 * (k + 1)] = onehot(isub == srow[0:1, 128 * k : 128 * (k + 1)])
-    def gather_senders(c, _):
-        rows = pl.ds(pl.multiple_of(c * SCH, 16), SCH)
-        pick = metac[rows, 64:65]
-        sc[rows, :] = dot_nn(onehot(iota((SCH, GRID), 1) == pick), grid[...]).astype(BF16)
-        return 0
-
-    lax.fori_loop(0, NCOMP // SCH, gather_senders, 0)
-    stage2(0)
-    stage0(1)
-    weights_ready(0)
-    for c in t_copies:
-        c.wait_recv()
-    lane = lax.broadcasted_iota(jnp.int32, (8, 128), 1)
-    for j in range(4):
-        even, odd = tbr[2 * j], tbr[2 * j + 1]
-        vecs[:, 128 * j : 128 * (j + 1)] = jnp.where(lane < LW, even, odd)
-
-    def full(k):
-        return wfull[:, k].reshape(LAT, LAT)
-
-    def first(c, _):
-        rows = pl.ds(pl.multiple_of(c * FCH, 16), FCH)
-        prec[rows, :] = (dot_nt(xc[rows, :], full(0)) + dot_nt(sc[rows, :], full(1)) + vecs[0:1, :]).astype(BF16)
-        return 0
-
-    lax.fori_loop(0, NCOMP // FCH, first, 0)
-
-    def arrange(c, _):
-        rows = pl.ds(pl.multiple_of(c * PCH, 16), PCH)
-        j0 = (c * PCH).astype(F32)
-        pre[rows, :] = dot_nn(onehot(iota((PCH, NCOMP), 0) + j0 == pcrow[0:1, :]), prec[...])
-        return 0
-
-    lax.fori_loop(0, NROW // PCH, arrange, 0)
-
-    def mlp(start, n):
-        rows = slice(start, start + n)
-        v = pre[rows, :] + dot_nt(recvrows[rows, :], full(2))
-        hid = silu(v).astype(BF16)
-        msg = norm_rows(dot_nn(hid, full(3)) + vecs[1:2, :], vecs[2:3, :], vecs[3:4, :])
-        msgb[rows, :] = msg.astype(BF16)
-    stage1(1)
-    mlp(base_of(0), C_OWN // 2)
-    mlp(base_of(0) + C_OWN // 2, C_OWN // 2)
-    mrecv[ownr, :] = msgb[ownr, :]
-    m_copies = []
-    g_wait = dict(zip(order, g_copies))
-    for gi, group in enumerate(GROUPS):
-        for s in group:
-            g_wait[s].wait_recv()
-        start = base_of(group[0])
-        n = sum(cap_of(s) for s in group)
-        mlp(start, n // 2)
-        mlp(start + n // 2, n - n // 2)
-        for s in group:
-            rows = pl.ds(base_of(s), cap_of(s))
-            c = remote(msgb.at[rows], mrecv.at[rows], m_ss.at[s], m_rs.at[s], (pp(s), h))
-            c.start()
-            m_copies.append(c)
-    stage2(1)
-
-
-    def scatter_block(c, _):
-        rows = pl.ds(pl.multiple_of(c * SCH, 16), SCH)
-        perm = onehot(iota((SCH, NROW), 1) == metac[rows, 0:1])
-        eoc[rows, :] = (xc[rows, :].astype(F32) + dot_nn(perm, msgb[...])).astype(BF16)
-        return 0
-
-    lax.fori_loop(0, NCOMP // SCH, scatter_block, 0)
-    low = lax.broadcasted_iota(jnp.int32, (HALF, 128), 1) < LW
-    for j in range(4):
-        cols = slice(128 * j, 128 * (j + 1))
-        top = eoc[0:HALF, cols].astype(F32)
-        bottom = eoc[HALF:NCOMP, cols].astype(F32)
-        xs[2 * j] = jnp.where(low, top, pltpu.roll(bottom, LW, 1)).astype(BF16)
-        xs[2 * j + 1] = jnp.where(low, pltpu.roll(top, LW, 1), bottom).astype(BF16)
-    x_copies = []
-    for half in range(2):
-        part = pl.ds(half * HALF // 2, HALF // 2)
-        for d in range(1, NH):
-            i = half * 8 + d
-            c = remote(xs.at[hp(d), part], xr.at[h, part], x_ss.at[i], x_rs.at[i], (p, hp(d)))
-            c.start()
-            x_copies.append(c)
-    xr[h] = xs[h]
 
     i8 = iota((8, 128), 0)
 
@@ -484,12 +372,140 @@
         return 0
 
     lax.fori_loop(0, 8, place2, 0)
+    got(reqr.at[1:NP], 2)
+    for s in range(NP):
+        b, c = base_of(s), cap_of(s)
+        for j in range(-(-c // 128)):
+            n = min(128, c - 128 * j)
+            srow[0:1, b + 128 * j : b + 128 * j + n] = reqr[s, j : j + 1, 0:n]
+    flag_p = jnp.max(reqr[:, 7, :], axis=0, keepdims=True)
+    flagr[h] = jnp.broadcast_to(flag_p, (8, 128))
+    il640 = iota((128, SUB), 1)
+    order = sum(GROUPS, ())
+    ownr = slice(base_of(0), base_of(0) + C_OWN)
+    g_copies = []
+
+    def pick_rows(lo, hi):
+        for k in range(lo, hi):
+            soh[128 * k : 128 * (k + 1), :] = onehot(il640 == col_of(srow[0:1, 128 * k : 128 * (k + 1)]))
+
+    ready = 0
+    for gi, group in enumerate(GROUPS):
+        upto = -(-(base_of(group[-1]) + cap_of(group[-1])) // 128)
+        pick_rows(ready, upto)
+        ready = upto
+        b = base_of(group[0])
+        n = sum(cap_of(s) for s in group)
+        serve[b : b + n, :] = dot_nn(soh[b : b + n, :], blk[...]).astype(BF16)
+        for s in group:
+            rows = pl.ds(base_of(s), cap_of(s))
+            c = remote(
+                serve.at[rows], recvrows.at[rows], snd.at[5], rcv.at[4 + gi], (lax.rem(p + NP - s, NP), h)
+            )
+            c.start()
+            g_copies.append(c)
+    fl_copies = [
+        remote(flagr.at[h], flagr.at[h], snd.at[9], rcv.at[3], (p, hp(d))) for d in range(1, NH)
+    ]
+    for c in fl_copies:
+        c.start()
+    stage1(1)
+    stage0(2)
+    pick_rows(ready, NROW // 128)
+    recvrows[ownr, :] = dot_nn(soh[ownr, :], blk[...]).astype(BF16)
+    isub = iota((SUB, 128), 0)
+    for k in range(NROW // 128):
+        scoh[:, 128 * k : 128 * (k + 1)] = onehot(isub == srow[0:1, 128 * k : 128 * (k + 1)])
+    def gather_senders(c, _):
+        rows = pl.ds(pl.multiple_of(c * SCH, 16), SCH)
+        pick = metac[rows, 64:65]
+        sc[rows, :] = dot_nn(onehot(iota((SCH, GRID), 1) == pick), grid[...]).astype(BF16)
+        return 0
+
+    lax.fori_loop(0, 2, gather_senders, 0)
+    stage2(0)
+    lax.fori_loop(2, NCOMP // SCH, gather_senders, 0)
+    stage2(1)
+    weights_ready(0)
+    got(tbr.at[1:NH], 1)
+    lane = lax.broadcasted_iota(jnp.int32, (8, 128), 1)
+    for j in range(4):
+        even, odd = tbr[2 * j], tbr[2 * j + 1]
+        vecs[:, 128 * j : 128 * (j + 1)] = jnp.where(lane < LW, even, odd)
+
+    def full(k):
+        return wfull[:, k].reshape(LAT, LAT)
+
+    def first(c, _):
+        rows = pl.ds(pl.multiple_of(c * FCH, 16), FCH)
+        prec[rows, :] = (dot_nt(xc[rows, :], full(0)) + dot_nt(sc[rows, :], full(1)) + vecs[0:1, :]).astype(BF16)
+        return 0
+
+    lax.fori_loop(0, NCOMP // FCH, first, 0)
+
+    def arrange(c, _):
+        rows = pl.ds(pl.multiple_of(c * PCH, 16), PCH)
+        j0 = (c * PCH).astype(F32)
+        pre[rows, :] = dot_nn(onehot(iota((PCH, NCOMP), 0) + j0 == pcrow[0:1, :]), prec[...])
+        return 0
+
+    lax.fori_loop(0, NROW // PCH, arrange, 0)
+
+    def mlp(start, n):
+        rows = slice(start, start + n)
+        v = pre[rows, :] + dot_nt(recvrows[rows, :], full(2))
+        hid = silu(v).astype(BF16)
+        msg = norm_rows(dot_nn(hid, full(3)) + vecs[1:2, :], vecs[2:3, :], vecs[3:4, :])
+        msgb[rows, :] = msg.astype(BF16)
+    weights_ready(1)
+    stage1(2)
+    mlp(base_of(0), C_OWN // 2)
+    mlp(base_of(0) + C_OWN // 2, C_OWN // 2)
+    mrecv[ownr, :] = msgb[ownr, :]
+    m_copies = []
+    for gi, group in enumerate(GROUPS):
+        start = base_of(group[0])
+        n = sum(cap_of(s) for s in group)
+        got(recvrows.at[start : start + n], 4 + gi)
+        start = base_of(group[0])
+        n = sum(cap_of(s) for s in group)
+        mlp(start, n // 2)
+        mlp(start + n // 2, n - n // 2)
+        for s in group:
+            rows = pl.ds(base_of(s), cap_of(s))
+            c = remote(msgb.at[rows], mrecv.at[rows], snd.at[6], rcv.at[7 + gi // 2], (pp(s), h))
+            c.start()
+            m_copies.append(c)
+
+
+    def scatter_block(c, _):
+        rows = pl.ds(pl.multiple_of(c * SCH, 16), SCH)
+        perm = onehot(iota((SCH, NROW), 1) == metac[rows, 0:1])
+        eoc[rows, :] = (xc[rows, :].astype(F32) + dot_nn(perm, msgb[...])).astype(BF16)
+        return 0
+
+    x_copies = []
+    low = lax.broadcasted_iota(jnp.int32, (HALF // 2, 128), 1) < LW
+    for half in range(2):
+        scatter_block(jnp.int32(half), 0)
+        scatter_block(jnp.int32(half + 2), 0)
+        part = pl.ds(half * HALF // 2, HALF // 2)
+        for j in range(4):
+            cols = slice(128 * j, 128 * (j + 1))
+            top = eoc[part, cols].astype(F32)
+            bottom = eoc[pl.ds(HALF + half * HALF // 2, HALF // 2), cols].astype(F32)
+            xs[2 * j, part, :] = jnp.where(low, top, pltpu.roll(bottom, LW, 1)).astype(BF16)
+            xs[2 * j + 1, part, :] = jnp.where(low, pltpu.roll(top, LW, 1), bottom).astype(BF16)
+        for d in range(1, NH):
+            c = remote(xs.at[hp(d), part], xr.at[h, part], snd.at[7], rcv.at[9 + half], (p, hp(d)))
+            c.start()
+            x_copies.append(c)
+    xr[h] = xs[h]
+
     lane_low = lax.broadcasted_iota(jnp.int32, (UCH, 128), 1) < LW
 
     def rows_arrived(half):
-        for d in range(1, NH):
-            src = xr.at[lax.rem(h + NH - d, NH), pl.ds(half * HALF // 2, HALF // 2)]
-            remote(src, src, x_ss.at[half * 8 + d], x_rs.at[half * 8 + d], (p, hp(d))).wait_recv()
+        got(xr.at[1:NH, pl.ds(half * HALF // 2, HALF // 2)], 9 + half)
 
     def edge_rows(t, _):
         b = t // (BLK // UCH)
@@ -512,62 +528,72 @@
         return 0
 
     per_half = 2 * (BLK // UCH)
-
-    for c in m_copies:
-        c.wait_recv()
-    weights_ready(1)
+    stage2(2)
+    got(mrecv.at[0 : base_of(1)], 7)
+    first_k = 768
     for c in range(2):
         rows = slice(c * SUB // 2, (c + 1) * SUB // 2)
-        summed[rows, :] = dot_nn(scoh[rows, :], mrecv[...]).astype(BF16)
-
-    def mesh(c, _):
+        mrow[rows, :] = dot_nn(scoh[rows, ownr], mrecv[ownr, :]) + dot_nn(scoh[rows, 0:first_k], mrecv[0:first_k, :])
+    weights_ready(2)
+
+    def mesh_first(c, _):
         rows = pl.ds(pl.multiple_of(c * (SUB // 2), 16), SUB // 2)
-        x = blk[rows, :]
-        v = dot_nt(x, full(4)) + dot_nt(summed[rows, :], full(5)) + vecs[4:5, :]
+        mpre[rows, :] = dot_nt(blk[rows, :], full(4)) + vecs[4:5, :]
+        return 0
+
+    lax.fori_loop(0, 2, mesh_first, 0)
+    got(mrecv.at[base_of(1) : base_of(0)], 8)
+    mo_copies = []
+    mo_own = []
+    for i, (start, n) in enumerate(((0, 256), (256, 384))):
+        rows = slice(start, start + n)
+        rest = slice(first_k, base_of(0))
+        total = (mrow[rows, :] + dot_nn(scoh[rows, rest], mrecv[rest, :])).astype(BF16)
+        v = mpre[rows, :] + dot_nt(total, full(5))
         hid = silu(v).astype(BF16)
         upd = norm_rows(dot_nn(hid, full(6)) + vecs[5:6, :], vecs[6:7, :], vecs[7:8, :])
-        mrow[rows, :] = x.astype(F32) + upd
-        return 0
-
-    lax.fori_loop(0, 2, mesh, 0)
-
-    def turn(c, _):
-        rows = pl.ds(pl.multiple_of(c * 128, 128), 128)
-        mot[:, rows] = mrow[rows, :].T.astype(BF16)
-        return 0
-
-    lax.fori_loop(0, SUB // 128, turn, 0)
-    mo_copies = []
-    at_mesh = pl.ds(pl.multiple_of(h * SUB, 128), SUB)
-    for d in range(1, NH):
-        c = remote(
-            mot.at[pl.ds(pl.multiple_of(hp(d) * LW, LW), LW), :], mo_hbm.at[:, at_mesh],
-            mo_ss.at[d], mo_rs.at[d], (p, hp(d)),
+        mrow[rows, :] = blk[rows, :].astype(F32) + upd
+        for k in range(start // 128, (start + n) // 128):
+            lanes = slice(128 * k, 128 * (k + 1))
+            mot[:, lanes] = mrow[lanes, :].T.astype(BF16)
+        at = pl.ds(pl.multiple_of(h * SUB + start, 128), n)
+        for d in range(1, NH):
+            c = remote(
+                mot.at[pl.ds(pl.multiple_of(hp(d) * LW, LW), LW), pl.ds(start, n)], mo_hbm.at[:, at],
+                snd.at[8], rcv.at[11], (p, hp(d)),
+            )
+            c.start()
+            mo_copies.append(c)
+        c = pltpu.make_async_copy(
+            mot.at[pl.ds(pl.multiple_of(h * LW, LW), LW), pl.ds(start, n)], mo_hbm.at[:, at], lsem.at[4]
         )
         c.start()
-        mo_copies.append(c)
-    mo_own = pltpu.make_async_copy(
-        mot.at[pl.ds(pl.multiple_of(h * LW, LW), LW), :], mo_hbm.at[:, at_mesh], lsem.at[3]
-    )
-    mo_own.start()
+        mo_own.append(c)
+
+    got(flagr.at[1:NH], 3)
+    flag_v[...] = jnp.max(flagr[...], axis=0)
+    flag_copy = pltpu.make_async_copy(flag_v, flag_hbm, lsem.at[6])
+    flag_copy.start()
     rows_arrived(0)
     lax.fori_loop(0, per_half, edge_rows, 0)
     rows_arrived(1)
     lax.fori_loop(per_half, 2 * per_half, edge_rows, 0)
-    eo_own = pltpu.make_async_copy(eot, eo_hbm, lsem.at[4])
+    eo_own = pltpu.make_async_copy(eot, eo_hbm, lsem.at[5])
     eo_own.start()
-    for d in range(1, NH):
-        src = lax.rem(h + NH - d, NH)
-        remote(flagr.at[src], flagr.at[src], fl_ss.at[d], fl_rs.at[d], (p, hp(d))).wait_recv()
-    flag_ref[...] = jnp.max(flagr[...], axis=0)
-    for c in t_copies + w_copies + q_copies + g_copies + fl_copies + m_copies + x_copies + mo_copies:
-        c.wait_send()
-    for d in range(1, NH):
-        src_h = lax.rem(h + NH - d, NH)
-        at_m = pl.ds(pl.multiple_of(src_h * SUB, 128), SUB)
-        remote(mo_hbm.at[:, at_m], mo_hbm.at[:, at_m], mo_ss.at[d], mo_rs.at[d], (p, hp(d))).wait_recv()
-    mo_own.wait()
+    sent(own_half, 0)
+    sent(tbr.at[1:NH], 1)
+    sent(wfull.at[0:3], 2)
+    sent(wfull.at[0:4], 3)
+    sent(req.at[1:NP], 4)
+    sent(serve.at[0 : base_of(0)], 5)
+    sent(msgb.at[0 : base_of(0)], 6)
+    sent(xs.at[1:NH], 7)
+    sent(mot.at[LW:LAT], 8)
+    sent(flagr.at[1:NH], 9)
+    got(mo_hbm.at[:, SUB:MESH], 11)
+    pltpu.make_async_copy(mot.at[0:LW], mot.at[0:LW], lsem.at[4]).wait()
     eo_own.wait()
+    flag_copy.wait()
 
 
 def sparse_step(grid_latent, mesh_latent, edge_latent, senders, receivers, mesh_slot, edge_counts,
@@ -592,10 +618,8 @@
         V((8, NROW), F32), V((NROW, SUB), BF16), V((NROW, LAT), BF16), V((NROW, LAT), BF16),
         V((SUB, NROW), BF16), V((NROW, LAT), BF16), V((NROW, LAT), BF16),
         V((8, NCOMP), F32), V((NCOMP, LAT), BF16), V((NH, HALF, 128), BF16), V((NH, HALF, 128), BF16),
-        V((LAT, SUB), BF16), V((LW, EDGE), BF16), V((SUB, LAT), BF16), V((SUB, LAT), F32), V((8, LAT), F32), V((NH, 8, 128), F32),
-        dma((5,)), dma((7,)), dma((8,)), dma((8,)), dma((8,)), dma((8,)), dma((8,)), dma((8,)),
-        dma((16,)), dma((16,)), dma((16,)), dma((16,)), dma((16,)), dma((16,)),
-        dma((16,)), dma((16,)), dma((8,)), dma((8,)), dma((8,)), dma((8,)),
+        V((LAT, SUB), BF16), V((LW, EDGE), BF16), V((SUB, LAT), F32), V((SUB, LAT), F32), V((8, LAT), F32), V((NH, 8, 128), F32), V((8, 128), F32),
+        dma((7,)), dma((10,)), dma((21,)),
     ]
     mo_t, eo_t, flag = pl.pallas_call(
         kernel,
@@ -606,7 +630,7 @@
         ),
         in_specs=[vm, vm, vm, pl.BlockSpec(memory_space=pltpu.SMEM), anyspec, anyspec, anyspec]
         + [anyspec] * 7 + [vm] * 8,
-        out_specs=(anyspec, anyspec, vm),
+        out_specs=(anyspec, anyspec, anyspec),
         scratch_shapes=scratch,
         compiler_params=pltpu.CompilerParams(
             collective_id=0, has_side_effects=True, vmem_limit_bytes=62 * 1024 * 1024

time: 80.5 us -> 75.4 us (0.937)
  the two profiles are of different devices: /device:TPU:1 before, /device:TPU:9 now
where the time goes in v3:
time: 75.4 us; the launch traced here: 75.2 us
  Pallas kernels  70 us (93%)
  local copies, waits for them, and re-layouts  3.01 us (4%)
  between operations  1.96 us (3%)
    pallas_call x1, Pallas kernels, sparse_step(): pl.pallas_call(kernel, out_shape=(jax.ShapeDtypeStruct((LW, MESH), BF16),...  70 us
    unnamed x4, local copies, waits for them, and re-layouts  1.81 us

profile of v3, /device:TPU:9, one launch (start us, length us, event | category | flops | bytes accessed | tf_op | source)
XLA Modules:
  0.0 75.2 jit_solution(7381130405429935804)
XLA Ops:
  1.3 0.0 copy-start
  1.3 70.0 %encoder.1 = (bf16[64,5120]{1,0:T(8,128)(2,1)S(1)}, bf16[64,8192]{1,0:T(8,128)(2,1)S(1)}, f32[8,128]{1,0:T(8,128)}) custom-call(s32[64,128]{1,0:T(8,128)} %bitcast.57, s32[64,128]{1,0:T(8,128)} %bitcast.58, s32[640,128]{1,0:T(8,128)} %bitcast.49, s32[1]{0:T(128)S(6)} %copy.142.cnt, bf16[8192,512]{1,0:T(8,128)(2,1)} %el_hbm.1, bf16[3072,512]{1,0:T(8,128)(2,1)} %grid_hbm.1, ...), custom_call_target="tpu_custom_call" | custom-call | tf_op jit(solution)/shard_map/encoder/pallas_call | solution.py:624
  71.3 1.2 %slice.3 = f32[1,1]{1,0:T(1,128)} slice(f32[8,128]{1,0:T(8,128)} %get-tuple-element.77), slice={[0:1], [0:1]} | slice | bytes 8 | tf_op jit(solution)/shard_map/slice | solution.py:709
  73.1 0.0 copy-done
  73.1 0.3 conditional.1
  73.4 0.8 %copy.143 = bf16[5120,64]{0,1:T(8,128)(2,1)} copy(bf16[5120,64]{0,1:T(8,128)(2,1)S(1)} %bitcast.56) | data formatting | bytes 1310720
  74.3 1.0 %copy.144 = bf16[8192,64]{0,1:T(8,128)(2,1)} copy(bf16[8192,64]{0,1:T(8,128)(2,1)S(1)} %bitcast.55) | data formatting | bytes 2097152
Async XLA Ops:
  1.3 71.9 %copy-start = (s32[81920]{0:T(1024)S(1)}, s32[81920]{0:T(1024)}, u32[]{:S(2)}) copy-start(s32[81920]{0:T(1024)} %param.29) | copy-start | bytes 983044

commit v4 on v3

--- a/solution.py
+++ b/solution.py
@@ -31,7 +31,8 @@
 HALF = NCOMP // 2
 DEV = pl.DeviceIdType.MESH
 PARTS = ((0, 2), (2, 2), (4, 3))
-GROUPS = ((5, 6, 7, 8, 9, 10, 11), (2, 3, 4, 12, 13, 14), (1, 15))
+GROUPS = ((5, 6, 7, 8, 9, 10, 11), (2, 3, 4, 12, 13, 14), (1,), (15,))
+G_SEM = (4, 5, 6, 21)
 
 
 def base_of(s):
@@ -91,11 +92,11 @@
     recv_i, send_i, slot, cnt, el_hbm, grid_hbm, mesh_hbm,
     w0, w1, w2, w3, w4, w5, w6,
     b0, b1, b2, b3, b4, b5, b6, b7,
-    mo_hbm, eo_hbm, flag_hbm,
+    mo_hbm, eo_hbm, flag_out,
     el, grid, blk, wfull, tb, tbr, oh, tabt, t_ref, s_ref, sub_ref, r_ref, sd_ref, m_ref, rk_ref, o_ref,
     posb, posc, aq, bq, req_acc, req, reqr, m2_ref, posx,
     xc, sc, prec, metac, pre, srow, soh, serve, recvrows, scoh, msgb, mrecv, pcrow, eoc, xs, xr,
-    mot, eot, mpre, mrow, vecs, flagr, flag_v,
+    mot, eot, mpre, mrow, vecs, flagr, flag_s,
     lsem, snd, rcv,
 ):
     p = lax.axis_index("patch")
@@ -248,7 +249,7 @@
     shift = q - pf
     shift = jnp.where(shift < 0.0, shift + NP, shift)
     eidx = lax.broadcasted_iota(jnp.int32, (64, 128), 0) * 128 + lax.broadcasted_iota(jnp.int32, (64, 128), 1)
-    live = eidx < cnt[0]
+    live = eidx < jnp.broadcast_to(cnt[...], (64, 128))
     own = live & (sub == hf)
     s_ref[...] = jnp.where(own, shift, -1.0)
     r_ref[...] = r1
@@ -400,7 +401,7 @@
         for s in group:
             rows = pl.ds(base_of(s), cap_of(s))
             c = remote(
-                serve.at[rows], recvrows.at[rows], snd.at[5], rcv.at[4 + gi], (lax.rem(p + NP - s, NP), h)
+                serve.at[rows], recvrows.at[rows], snd.at[5], rcv.at[G_SEM[gi]], (lax.rem(p + NP - s, NP), h)
             )
             c.start()
             g_copies.append(c)
@@ -466,11 +467,11 @@
     for gi, group in enumerate(GROUPS):
         start = base_of(group[0])
         n = sum(cap_of(s) for s in group)
-        got(recvrows.at[start : start + n], 4 + gi)
+        got(recvrows.at[start : start + n], G_SEM[gi])
         start = base_of(group[0])
         n = sum(cap_of(s) for s in group)
-        mlp(start, n // 2)
-        mlp(start + n // 2, n - n // 2)
+        for k in range(0, n, 224):
+            mlp(start + k, min(224, n - k))
         for s in group:
             rows = pl.ds(base_of(s), cap_of(s))
             c = remote(msgb.at[rows], mrecv.at[rows], snd.at[6], rcv.at[7 + gi // 2], (pp(s), h))
@@ -571,8 +572,8 @@
         mo_own.append(c)
 
     got(flagr.at[1:NH], 3)
-    flag_v[...] = jnp.max(flagr[...], axis=0)
-    flag_copy = pltpu.make_async_copy(flag_v, flag_hbm, lsem.at[6])
+    flag_s[0] = jnp.max(jnp.max(flagr[...], axis=0)).astype(jnp.int32)
+    flag_copy = pltpu.make_async_copy(flag_s, flag_out, lsem.at[6])
     flag_copy.start()
     rows_arrived(0)
     lax.fori_loop(0, per_half, edge_rows, 0)
@@ -618,17 +619,17 @@
         V((8, NROW), F32), V((NROW, SUB), BF16), V((NROW, LAT), BF16), V((NROW, LAT), BF16),
         V((SUB, NROW), BF16), V((NROW, LAT), BF16), V((NROW, LAT), BF16),
         V((8, NCOMP), F32), V((NCOMP, LAT), BF16), V((NH, HALF, 128), BF16), V((NH, HALF, 128), BF16),
-        V((LAT, SUB), BF16), V((LW, EDGE), BF16), V((SUB, LAT), F32), V((SUB, LAT), F32), V((8, LAT), F32), V((NH, 8, 128), F32), V((8, 128), F32),
-        dma((7,)), dma((10,)), dma((21,)),
+        V((LAT, SUB), BF16), V((LW, EDGE), BF16), V((SUB, LAT), F32), V((SUB, LAT), F32), V((8, LAT), F32), V((NH, 8, 128), F32), pltpu.SMEM((1,), jnp.int32),
+        dma((7,)), dma((10,)), dma((22,)),
     ]
     mo_t, eo_t, flag = pl.pallas_call(
         kernel,
         out_shape=(
             jax.ShapeDtypeStruct((LW, MESH), BF16),
             jax.ShapeDtypeStruct((LW, EDGE), BF16),
-            jax.ShapeDtypeStruct((8, 128), F32),
+            jax.ShapeDtypeStruct((1,), jnp.int32),
         ),
-        in_specs=[vm, vm, vm, pl.BlockSpec(memory_space=pltpu.SMEM), anyspec, anyspec, anyspec]
+        in_specs=[vm, vm, vm, vm, anyspec, anyspec, anyspec]
         + [anyspec] * 7 + [vm] * 8,
         out_specs=(anyspec, anyspec, anyspec),
         scratch_shapes=scratch,
@@ -636,7 +637,7 @@
             collective_id=0, has_side_effects=True, vmem_limit_bytes=62 * 1024 * 1024
         ),
         name="encoder",
-    )(receivers.reshape(64, 128), senders.reshape(64, 128), mesh_slot.reshape(TAB, 128), edge_counts,
+    )(receivers.reshape(64, 128), senders.reshape(64, 128), mesh_slot.reshape(TAB, 128), edge_counts.reshape(1, 1),
       edge_latent, grid_latent, mesh_latent, *weights, *vectors)
     return mo_t, eo_t, flag
 
@@ -706,7 +707,7 @@
         mo, eo = general_step(*args)
         return jnp.zeros_like(state[0]), mo, eo
 
-    mo_t, eo_t = lax.cond(flag[0, 0] > 0.5, lambda: general_step(*args), lambda: (mo_t, eo_t))
+    mo_t, eo_t = lax.cond(flag[0] > 0, lambda: general_step(*args), lambda: (mo_t, eo_t))
     return mo_t.T, eo_t.T
 
 

time: 75.4 us -> 73.6 us (0.976)
  local copies, waits for them, and re-layouts: 3.01 us -> 1.81 us
    slice x1 -> x0, local copies, waits for them, and re-layouts: 1.19 us -> none  [step(): flag[0, 0] > 0.5]
where the time goes in v4:
time: 73.6 us; the launch traced here: 73.4 us
  Pallas kernels  69.4 us (94%)
  between operations  2 us (3%)
  local copies, waits for them, and re-layouts  1.81 us (2%)
    pallas_call x1, Pallas kernels, sparse_step(): pl.pallas_call(kernel, out_shape=(jax.ShapeDtypeStruct((LW, MESH), BF16),...  69.4 us
    unnamed x4, local copies, waits for them, and re-layouts  1.81 us

profile of v4, /device:TPU:9, one launch (start us, length us, event | category | flops | bytes accessed | tf_op | source)
XLA Modules:
  0.0 73.4 jit_solution(6601343234886372131)
XLA Ops:
  1.3 0.0 copy-start
  1.3 69.4 %encoder.1 = (bf16[64,5120]{1,0:T(8,128)(2,1)S(1)}, bf16[64,8192]{1,0:T(8,128)(2,1)S(1)}, s32[1]{0:T(128)}) custom-call(s32[64,128]{1,0:T(8,128)} %bitcast.59, s32[64,128]{1,0:T(8,128)} %bitcast.60, s32[640,128]{1,0:T(8,128)} %bitcast.51, s32[1,1]{1,0:T(1,128)} %bitcast.50.cnt, bf16[8192,512]{1,0:T(8,128)(2,1)} %el_hbm.1, bf16[3072,512]{1,0:T(8,128)(2,1)} %grid_hbm.1, ...), custom_call_target="tpu_custom_call" | custom-call | tf_op jit(solution)/shard_map/encoder/pallas_call | solution.py:625
  71.3 0.0 copy-done
  71.4 0.3 conditional.1
  71.6 0.8 %copy.143 = bf16[5120,64]{0,1:T(8,128)(2,1)} copy(bf16[5120,64]{0,1:T(8,128)(2,1)S(1)} %bitcast.58) | data formatting | bytes 1310720
  72.5 1.0 %copy.144 = bf16[8192,64]{0,1:T(8,128)(2,1)} copy(bf16[8192,64]{0,1:T(8,128)(2,1)S(1)} %bitcast.57) | data formatting | bytes 2097152
Async XLA Ops:
  1.3 70.1 %copy-start = (s32[81920]{0:T(1024)S(1)}, s32[81920]{0:T(1024)}, u32[]{:S(2)}) copy-start(s32[81920]{0:T(1024)} %param.29) | copy-start | bytes 983044

commit v5 on v4

--- a/solution.py
+++ b/solution.py
@@ -31,6 +31,8 @@
 HALF = NCOMP // 2
 DEV = pl.DeviceIdType.MESH
 PARTS = ((0, 2), (2, 2), (4, 3))
+FAR_FIRST = (4, 3, 5, 2, 6, 7, 1)
+HOPS = (10, 6, 9, 11, 14, 2, 7, 8, 13, 3, 5, 12, 4, 1, 15)
 GROUPS = ((5, 6, 7, 8, 9, 10, 11), (2, 3, 4, 12, 13, 14), (1,), (15,))
 G_SEM = (4, 5, 6, 21)
 
@@ -398,7 +400,7 @@
         b = base_of(group[0])
         n = sum(cap_of(s) for s in group)
         serve[b : b + n, :] = dot_nn(soh[b : b + n, :], blk[...]).astype(BF16)
-        for s in group:
+        for s in sorted(group, key=HOPS.index):
             rows = pl.ds(base_of(s), cap_of(s))
             c = remote(
                 serve.at[rows], recvrows.at[rows], snd.at[5], rcv.at[G_SEM[gi]], (lax.rem(p + NP - s, NP), h)
@@ -472,7 +474,7 @@
         n = sum(cap_of(s) for s in group)
         for k in range(0, n, 224):
             mlp(start + k, min(224, n - k))
-        for s in group:
+        for s in sorted(group, key=HOPS.index):
             rows = pl.ds(base_of(s), cap_of(s))
             c = remote(msgb.at[rows], mrecv.at[rows], snd.at[6], rcv.at[7 + gi // 2], (pp(s), h))
             c.start()
@@ -497,7 +499,7 @@
             bottom = eoc[pl.ds(HALF + half * HALF // 2, HALF // 2), cols].astype(F32)
             xs[2 * j, part, :] = jnp.where(low, top, pltpu.roll(bottom, LW, 1)).astype(BF16)
             xs[2 * j + 1, part, :] = jnp.where(low, pltpu.roll(top, LW, 1), bottom).astype(BF16)
-        for d in range(1, NH):
+        for d in FAR_FIRST:
             c = remote(xs.at[hp(d), part], xr.at[h, part], snd.at[7], rcv.at[9 + half], (p, hp(d)))
             c.start()
             x_copies.append(c)
@@ -558,7 +560,7 @@
             lanes = slice(128 * k, 128 * (k + 1))
             mot[:, lanes] = mrow[lanes, :].T.astype(BF16)
         at = pl.ds(pl.multiple_of(h * SUB + start, 128), n)
-        for d in range(1, NH):
+        for d in FAR_FIRST:
             c = remote(
                 mot.at[pl.ds(pl.multiple_of(hp(d) * LW, LW), LW), pl.ds(start, n)], mo_hbm.at[:, at],
                 snd.at[8], rcv.at[11], (p, hp(d)),

time: 73.6 us -> 70.6 us (0.959)
  the two profiles are of different devices: /device:TPU:9 before, /device:TPU:1 now
where the time goes in v5:
time: 70.6 us; the launch traced here: 70.5 us
  Pallas kernels  66.4 us (94%)
  between operations  2 us (3%)
  local copies, waits for them, and re-layouts  1.81 us (3%)
    pallas_call x1, Pallas kernels, sparse_step(): pl.pallas_call(kernel, out_shape=(jax.ShapeDtypeStruct((LW, MESH), BF16),...  66.4 us
    unnamed x4, local copies, waits for them, and re-layouts  1.81 us

profile of v5, /device:TPU:1, one launch (start us, length us, event | category | flops | bytes accessed | tf_op | source)
XLA Modules:
  0.0 70.5 jit_solution(14078356136685194181)
XLA Ops:
  1.3 0.0 copy-start
  1.3 66.4 %encoder.1 = (bf16[64,5120]{1,0:T(8,128)(2,1)S(1)}, bf16[64,8192]{1,0:T(8,128)(2,1)S(1)}, s32[1]{0:T(128)}) custom-call(s32[64,128]{1,0:T(8,128)} %bitcast.59, s32[64,128]{1,0:T(8,128)} %bitcast.60, s32[640,128]{1,0:T(8,128)} %bitcast.51, s32[1,1]{1,0:T(1,128)} %bitcast.50.cnt, bf16[8192,512]{1,0:T(8,128)(2,1)} %el_hbm.1, bf16[3072,512]{1,0:T(8,128)(2,1)} %grid_hbm.1, ...), custom_call_target="tpu_custom_call" | custom-call | tf_op jit(solution)/shard_map/encoder/pallas_call | solution.py:627
  68.4 0.0 copy-done
  68.4 0.3 conditional.1
  68.6 0.8 %copy.143 = bf16[5120,64]{0,1:T(8,128)(2,1)} copy(bf16[5120,64]{0,1:T(8,128)(2,1)S(1)} %bitcast.58) | data formatting | bytes 1310720
  69.5 1.0 %copy.144 = bf16[8192,64]{0,1:T(8,128)(2,1)} copy(bf16[8192,64]{0,1:T(8,128)(2,1)S(1)} %bitcast.57) | data formatting | bytes 2097152
Async XLA Ops:
  1.3 67.1 %copy-start = (s32[81920]{0:T(1024)S(1)}, s32[81920]{0:T(1024)}, u32[]{:S(2)}) copy-start(s32[81920]{0:T(1024)} %param.29) | copy-start | bytes 983044
